TPU v7x, 256 devices: a whole 4x4x8 slice. The times are simulated.
256 devices in a mesh: clip: 8 (over x_lo, y), tile: 32 (over x_hi, z, core).
Axes of the slice: x: 4 (x_hi: 2, x_lo: 2; x = x_hi * 2 + x_lo), y: 4, z: 8, core: 2. Of those that a mesh axis runs over, the one named last changes fastest.
Arguments:
- clip_features: bfloat16 [8, 9, 96, 32, 128], P('clip', None, 'tile'), may hold values from -6 to 6
- upstream: bfloat16 [8, 9, 96, 32, 128], P('clip', None, 'tile'), may hold values from -3 to 3
- weight: bfloat16 [27, 128, 128], replicated, may hold values from -0.109375 to 0.109375
- conv_bias: float32 [128], replicated, may hold values from -2 to 2
Outputs:
- grad_weight: float32 [3456, 128], P('tile')
- grad_bias: float32 [128], replicated
- penalty: float32 [], replicated
All inputs are finite; a program needn't handle non-finite values.
Results may differ from a plain program's by a relative error of at most 0.002.
Values may be sent and summed in bfloat16 or wider, within the bound.
No kernel may reach another device: no remote copies, remote signals or barrier semaphores. Data moves between devices by JAX's collectives and lax.ppermute only.
A program may use at most 64 MiB of HBM per device.

v0:
```python
import jax
import jax.numpy as jnp
from jax import lax
from jax.sharding import PartitionSpec as P

r1_weight = 10.0


def padded_2(cells, sides, width):
    for axis, dim in sides:
        count = lax.axis_size(axis)
        ends = count - 1
        head = lax.slice_in_dim(cells, 0, width, axis=dim)
        tail = lax.slice_in_dim(cells, cells.shape[dim] - width, cells.shape[dim], axis=dim)
        cells = jnp.concatenate(
            [
                lax.ppermute(tail, axis, [(i, (i + 1) % count) for i in range(ends)]),
                cells,
                lax.ppermute(head, axis, [((i + 1) % count, i) for i in range(ends)]),
            ],
            axis=dim,
        )
    return cells


def cut_along(value, dim, count):
    before, after = (value.shape[:dim], value.shape[dim + 1 :])
    return jnp.moveaxis(value.reshape(*before, count, -1, *after), dim, 0)


def sent_and_summed(value, axis, dim):
    pieces = cut_along(value, dim, lax.axis_size(axis))
    arrived = lax.all_to_all(pieces, axis, split_axis=0, concat_axis=0, tiled=True)
    return arrived.sum(axis=0)


def in_one_piece(arrays, axis, dim, along):
    columns = [a.reshape(*a.shape[:along], -1) for a in arrays]
    both = jnp.concatenate(columns, axis=along)
    out, at, done = (sent_and_summed(both, axis, dim), 0, [])
    for a, column in zip(arrays, columns):
        section = out[..., at : at + column.shape[along]]
        done.append(section.reshape(*section.shape[:along], *a.shape[along:]))
        at += column.shape[along]
    return tuple(done)


def sent_to_all(value, axis):
    count = lax.axis_size(axis)
    return lax.all_to_all(
        jnp.broadcast_to(value[None], (count, *value.shape)), axis, 0, 0, tiled=True
    )


def over_copies(value, axis):
    everything = sent_to_all(value, axis)
    return jnp.sum(everything, axis=0)


def together(arrays, axis):
    vector, at, done = (jnp.concatenate([a.reshape(-1) for a in arrays]), 0, [])
    total = over_copies(vector, axis)
    for a in arrays:
        done.append(total[at : at + a.size].reshape(a.shape))
        at += a.size
    return tuple(done)


def slope_of(value):
    return 0.2 + 0.8 * jax.nn.sigmoid(value)


def bend_of(value):
    sigma = jax.nn.sigmoid(value)
    return 0.8 * sigma * (1.0 - sigma)


def pad_rest(field):
    return jnp.pad(field, ((0, 0), (1, 1), (0, 0), (1, 1), (0, 0)))


def conv_cells(padded, stacked, flipped):
    count, frame_pad, width_pad, row_pad, channels = padded.shape
    frames = frame_pad - 2
    columns = width_pad - 2
    row_count = row_pad - 2
    summed = jnp.zeros((count * frames * columns * row_count, stacked.shape[2]), jnp.float32)
    for tap_f in range(3):
        for tap_w in range(3):
            off_frame = 2 - tap_f if flipped else tap_f
            off_column = 2 - tap_w if flipped else tap_w
            pieces = []
            for tap_h in range(3):
                off_row = 2 - tap_h if flipped else tap_h
                pieces.append(
                    padded[
                        :,
                        off_frame : off_frame + frames,
                        off_column : off_column + columns,
                        off_row : off_row + row_count,
                        :,
                    ]
                )
            joined = jnp.concatenate(pieces, axis=-1).reshape(-1, 3 * channels)
            summed = summed + jnp.dot(
                joined, stacked[3 * tap_f + tap_w], preferred_element_type=jnp.float32
            )
    return summed.reshape(count, frames, columns, row_count, -1)


def wgrad_cells(pairs):
    partials = []
    for tap_f in range(3):
        for tap_w in range(3):
            left_parts = []
            right_parts = []
            for padded, gradients in pairs:
                count, frame_pad, width_pad, row_pad, channels = padded.shape
                frames = frame_pad - 2
                columns = width_pad - 2
                row_count = row_pad - 2
                pieces = [
                    padded[
                        :,
                        tap_f : tap_f + frames,
                        tap_w : tap_w + columns,
                        tap_h : tap_h + row_count,
                        :,
                    ]
                    for tap_h in range(3)
                ]
                left_parts.append(jnp.concatenate(pieces, axis=-1).reshape(-1, 3 * channels))
                right_parts.append(gradients.reshape(-1, gradients.shape[-1]))
            left_all = jnp.concatenate(left_parts, axis=0)
            right_all = jnp.concatenate(right_parts, axis=0)
            partials.append(
                lax.dot_general(
                    left_all,
                    right_all,
                    (((0,), (0,)), ((), ())),
                    preferred_element_type=jnp.float32,
                )
            )
    return jnp.concatenate(partials, axis=0)


def with_stats(terms, curvature, squares, tile_count):
    bias_local = jnp.sum(curvature.astype(jnp.float32), axis=(0, 1, 2, 3))
    bias_rows = jnp.broadcast_to(bias_local[None, :], (tile_count, bias_local.shape[0]))
    square_rows = jnp.broadcast_to(squares[None], (tile_count,))
    return (terms, bias_rows, square_rows)


def shards(clip_features, upstream, weight, conv_bias):
    count, frames, columns, row_count, channels = clip_features.shape
    stacked = weight.reshape(9, 3 * channels, channels)
    flipped = jnp.swapaxes(weight, 1, 2).reshape(9, 3 * channels, channels)
    tile_count = lax.axis_size("tile")
    width_all = columns * tile_count
    cell_total = count * lax.axis_size("clip") * frames * row_count * width_all
    factor = r1_weight / cell_total
    upstream_f = upstream.astype(jnp.float32)
    input_ext, upstream_ext = (
        padded_2(clip_features, (("tile", 2),), 3),
        padded_2(upstream, (("tile", 2),), 3),
    )
    hidden_ext = conv_cells(pad_rest(input_ext), stacked, False) + conv_bias
    grad_h_ext = (upstream_ext[:, :, 1:-1].astype(jnp.float32) * slope_of(hidden_ext)).astype(
        jnp.bfloat16
    )
    grad_x_ext = conv_cells(pad_rest(grad_h_ext), flipped, True)
    column = lax.axis_index("tile") * columns - 1 + jnp.arange(columns + 2)
    inside = ((column >= 0) & (column < width_all)).astype(jnp.float32)
    grad_x_ext = grad_x_ext * inside[None, None, :, None, None]
    grad_x = grad_x_ext[:, :, 1:-1]
    gradx_pad = pad_rest(grad_x_ext.astype(jnp.bfloat16))
    input_pad = pad_rest(input_ext[:, :, 2:-2])
    hidden = hidden_ext[:, :, 2:-2]
    grad_h = grad_h_ext[:, :, 2:-2]
    squares = jnp.sum(grad_x * grad_x)
    back_conv = conv_cells(gradx_pad, stacked, False)
    curvature = (back_conv * upstream_f * bend_of(hidden)).astype(jnp.bfloat16)
    payload = with_stats(
        wgrad_cells(((gradx_pad, grad_h), (input_pad, curvature))), curvature, squares, tile_count
    )
    reduced = (
        sent_and_summed(payload[0], "tile", 0),
        *in_one_piece((payload[1], payload[2]), "tile", 0, 1),
    )
    totals = together((reduced[0], reduced[1], reduced[2]), "clip")
    grad_weight = factor * totals[0]
    bias_sum = totals[1][0]
    square_sum = totals[2][0]
    return (grad_weight, factor * bias_sum, 0.5 * factor * square_sum)


def solution(mesh):
    in_specs = (P("clip", None, "tile", None, None), P("clip", None, "tile", None, None), P(), P())
    out_specs = (P("tile", None), P(), P())
    return jax.shard_map(shards, mesh=mesh, in_specs=in_specs, out_specs=out_specs, check_vma=False)
```

profile of v0, /device:TPU:32, one launch (start us, length us, event | category | flops | bytes accessed | tf_op | source)
XLA Modules:
  0.0 155.8 jit_solution(10422544349131577361)
XLA Ops:
  0.6 2.1 %collective-permute-start.2 = (bf16[1,9,3,32,128]{4,3,2,1,0:T(8,128)(2,1)}, bf16[1,9,3,32,128]{4,3,2,1,0:T(8,128)(2,1)S(1)}, u32[]{:S(2)}, u32[]{:S(2)}) collective-permute-start(bf16[1,9,3,32,128]{4,3,2,1,0:T(8,128)(2,1)} %param.4), channel_id=1, source_target_pairs={{0,1},{1,2},{2,3},{3,4},{4,5},{5,6},{6,7},{7,8},{8,9},{9,10},{10,1... | collective-permute-start | bytes 663560 | tf_op jit(solution)/shard_map/ppermute | solution.py:17
  2.7 3.6 %collective-permute-start.3 = (bf16[1,9,3,32,128]{4,3,2,1,0:T(8,128)(2,1)}, bf16[1,9,3,32,128]{4,3,2,1,0:T(8,128)(2,1)S(1)}, u32[]{:S(2)}, u32[]{:S(2)}) collective-permute-start(bf16[1,9,3,32,128]{4,3,2,1,0:T(8,128)(2,1)} %param.4), channel_id=1, source_target_pairs={{1,0},{2,1},{3,2},{4,3},{5,4},{6,5},{7,6},{8,7},{9,8},{10,9},{11,1... | collective-permute-start | bytes 663560 | tf_op jit(solution)/shard_map/ppermute | solution.py:19
  6.4 2.2 %collective-permute-start = (bf16[1,9,3,32,128]{4,3,2,1,0:T(8,128)(2,1)}, bf16[1,9,3,32,128]{4,3,2,1,0:T(8,128)(2,1)}, u32[]{:S(2)}, u32[]{:S(2)}) collective-permute-start(bf16[1,9,3,32,128]{4,3,2,1,0:T(8,128)(2,1)} %param.5), channel_id=1, source_target_pairs={{0,1},{1,2},{2,3},{3,4},{4,5},{5,6},{6,7},{7,8},{8,9},{9,10},{10,1... | collective-permute-start | bytes 663560 | tf_op jit(solution)/shard_map/ppermute | solution.py:17
  8.6 3.4 %collective-permute-start.1 = (bf16[1,9,3,32,128]{4,3,2,1,0:T(8,128)(2,1)}, bf16[1,9,3,32,128]{4,3,2,1,0:T(8,128)(2,1)}, u32[]{:S(2)}, u32[]{:S(2)}) collective-permute-start(bf16[1,9,3,32,128]{4,3,2,1,0:T(8,128)(2,1)} %param.5), channel_id=1, source_target_pairs={{1,0},{2,1},{3,2},{4,3},{5,4},{6,5},{7,6},{8,7},{9,8},{10,9},{11,1... | collective-permute-start | bytes 663560 | tf_op jit(solution)/shard_map/ppermute | solution.py:19
  11.9 1.3 fusion.83
  13.3 1.3 copy.9
  14.8 0.8 copy-done.25
  15.6 3.3 %pad_slice_fusion.2 = (bf16[1,9,7,32,128]{4,3,2,1,0:T(8,128)(2,1)S(1)}, bf16[1,9,7,32,128]{4,3,2,1,0:T(8,128)(2,1)S(1)}, bf16[1,9,7,32,128]{4,3,2,1,0:T(8,128)(2...) fusion(bf16[1,9,9,32,128]{4,3,2,1,0:T(8,128)(2,1)S(1)} %constan, ...), kind=kLoop, calls=%fused_computation.18 | loop fusion | bytes 10469376 | tf_op jit(solution)/shard_map/slice | solution.py:96
  19.0 0.7 pad_slice_fusion.1
  27.7 1.4 multiply_convert_fusion
  29.1 1.4 pad_slice_fusion.26
  37.4 0.9 pad_slice_fusion.74
  39.3 2.2 %pad_slice_fusion.50 = (bf16[1,9,3,32,128]{4,3,2,1,0:T(8,128)(2,1)}, bf16[1,9,3,32,128]{4,3,2,1,0:T(8,128)(2,1)}, bf16[1,9,3,32,128]{4,3,2,1,0:T(8,128)(2,1)}, b...) fusion(bf16[1,9,5,32,128]{4,3,2,1,0:T(8,128)(2,1)S(1)} %slice.627), kind=kLoop, calls=%fused_computation.111 | loop fusion | bytes 4571136 | tf_op jit(solution)/shard_map/slice | solution.py:123
  41.5 1.0 pad_slice_fusion.49
  43.0 0.7 fusion.67
  47.7 0.9 convert_reduce_fusion
  49.9 13.7 %all-to-all-start.1 = ((f32[32,1,129]{2,1,0:T(1,128)}), f32[32,1,129]{2,1,0:T(1,128)}, u32[]{:S(2)}, u32[]{:S(2)}) async-start(f32[32,1,129]{2,1,0:T(1,128)} %reshape.338), calls=%async_computation.1 | async-start | bytes 65536 | tf_op jit(solution)/shard_map/all_to_all | solution.py:33
  63.6 2.1 %fusion.64 = (bf16[1,9,3,32,384]{4,3,2,1,0:T(8,128)(2,1)S(1)}, bf16[1,9,3,32,384]{4,3,2,1,0:T(8,128)(2,1)S(1)}, bf16[1,9,3,32,384]{4,3,2,1,0:T(8,128)(2,1)S(1)}, bf16[1,9,3,32,384]{4,3,2,1,0:T(8,128)(2,1)S(1)}) fusion(bf16[1,9,3,32,128]{4,3,2,1,0:T(8,128)(2,1)} %copy-done.28, bf16[1,9,3,32,128]{4,3,2,1,0:T(8,128)(2,1)S(1)} %copy-done.26, ...), kind=kLoop, calls=%fused_computation.186 | loop fusion | flops 9289728 | bytes 5308416 | tf_op jit(solution)/shard_map/concatenate | solution.py:132
  65.8 1.3 fusion.60
  67.4 1.3 fusion.57
  68.6 1.3 fusion.54
  69.9 1.3 fusion.51
  71.2 1.3 fusion.48
  72.5 1.2 fusion.45
  74.1 1.3 fusion.42
  75.3 1.3 fusion.39
  76.8 1.3 fusion.36
  78.0 2.6 %reshape.336 = f32[32,108,128]{2,1,0:T(8,128)} reshape(f32[3456,128]{1,0:T(8,128)} %fusion.36) | data formatting | bytes 3538944 | tf_op jit(solution)/shard_map/reshape | solution.py:28
  80.6 9.8 %all-to-all-start = ((f32[32,108,128]{2,1,0:T(8,128)}), f32[32,108,128]{2,1,0:T(8,128)S(1)}, u32[]{:S(2)}, u32[]{:S(2)}) async-start(f32[32,108,128]{2,1,0:T(8,128)} %reshape.336), calls=%async_computation | async-start | bytes 3670016 | tf_op jit(solution)/shard_map/all_to_all | solution.py:33
  90.4 0.8 reduce_sum.50
  91.7 46.0 %all-to-all-done = f32[32,108,128]{2,1,0:T(8,128)S(1)} async-done(((f32[32,108,128]{2,1,0:T(8,128)}), f32[32,108,128]{2,1,0:T(8,128)S(1)}, u32[]{:S(2)}, u32[]{:S(2)}) %all-to-all-start) | async-done | bytes 1769504 | tf_op jit(solution)/shard_map/all_to_all | solution.py:33
  138.7 13.3 %all_to_all.16 = f32[8,1,13953]{2,1,0:T(1,128)S(1)} all-to-all(f32[8,1,13953]{2,1,0:T(1,128)S(1)} %broadcast_in_dim.2), channel_id=1, replica_groups=mesh['clip'=8,'tile'=32] {'clip'}, dimensions={0} | all-to-all | bytes 892992 | tf_op jit(solution)/shard_map/all_to_all | solution.py:50
  (142 shorter events, 25.9 us)
Async XLA Ops:
  0.6 12.6 %copy-start = (bf16[27,128,128]{2,1,0:T(8,128)(2,1)S(1)}, bf16[27,128,128]{2,1,0:T(8,128)(2,1)}, u32[]{:S(2)}) copy-start(bf16[27,128,128]{2,1,0:T(8,128)(2,1)} %param.6) | copy-start | bytes 2654212
  0.6 14.1 %collective-permute-start.2 = (bf16[1,9,3,32,128]{4,3,2,1,0:T(8,128)(2,1)}, bf16[1,9,3,32,128]{4,3,2,1,0:T(8,128)(2,1)S(1)}, u32[]{:S(2)}, u32[]{:S(2)}) collective-permute-start(bf16[1,9,3,32,128]{4,3,2,1,0:T(8,128)(2,1)} %param.4), channel_id=1, source_target_pairs={{0,1},{1,2},{2,3},{3,4},{4,5},{5,6},{6,7},{7,8},{8,9},{9,10},{10,1... | collective-permute-start | bytes 663560 | tf_op jit(solution)/shard_map/ppermute | solution.py:17
  2.7 12.9 %collective-permute-start.3 = (bf16[1,9,3,32,128]{4,3,2,1,0:T(8,128)(2,1)}, bf16[1,9,3,32,128]{4,3,2,1,0:T(8,128)(2,1)S(1)}, u32[]{:S(2)}, u32[]{:S(2)}) collective-permute-start(bf16[1,9,3,32,128]{4,3,2,1,0:T(8,128)(2,1)} %param.4), channel_id=1, source_target_pairs={{1,0},{2,1},{3,2},{4,3},{5,4},{6,5},{7,6},{8,7},{9,8},{10,9},{11,1... | collective-permute-start | bytes 663560 | tf_op jit(solution)/shard_map/ppermute | solution.py:19
  6.4 21.1 %collective-permute-start = (bf16[1,9,3,32,128]{4,3,2,1,0:T(8,128)(2,1)}, bf16[1,9,3,32,128]{4,3,2,1,0:T(8,128)(2,1)}, u32[]{:S(2)}, u32[]{:S(2)}) collective-permute-start(bf16[1,9,3,32,128]{4,3,2,1,0:T(8,128)(2,1)} %param.5), channel_id=1, source_target_pairs={{0,1},{1,2},{2,3},{3,4},{4,5},{5,6},{6,7},{7,8},{8,9},{9,10},{10,1... | collective-permute-start | bytes 663560 | tf_op jit(solution)/shard_map/ppermute | solution.py:17
  8.6 18.9 %collective-permute-start.1 = (bf16[1,9,3,32,128]{4,3,2,1,0:T(8,128)(2,1)}, bf16[1,9,3,32,128]{4,3,2,1,0:T(8,128)(2,1)}, u32[]{:S(2)}, u32[]{:S(2)}) collective-permute-start(bf16[1,9,3,32,128]{4,3,2,1,0:T(8,128)(2,1)} %param.5), channel_id=1, source_target_pairs={{1,0},{2,1},{3,2},{4,3},{5,4},{6,5},{7,6},{8,7},{9,8},{10,9},{11,1... | collective-permute-start | bytes 663560 | tf_op jit(solution)/shard_map/ppermute | solution.py:19
  14.6 0.9 copy-start.25
  14.7 4.3 %copy-start.27 = (bf16[1,9,3,32,128]{4,3,2,1,0:T(8,128)(2,1)}, bf16[1,9,3,32,128]{4,3,2,1,0:T(8,128)(2,1)S(1)}, u32[]{:S(2)}) copy-start(bf16[1,9,3,32,128]{4,3,2,1,0:T(8,128)(2,1)S(1)} %collective-permute-done.2) | copy-start | bytes 663556
  15.6 3.4 %copy-start.28 = (bf16[1,9,3,32,128]{4,3,2,1,0:T(8,128)(2,1)}, bf16[1,9,3,32,128]{4,3,2,1,0:T(8,128)(2,1)S(1)}, u32[]{:S(2)}) copy-start(bf16[1,9,3,32,128]{4,3,2,1,0:T(8,128)(2,1)S(1)} %collective-permute-done.3) | copy-start | bytes 663556
  47.7 15.9 %copy-start.26 = (bf16[1,9,3,32,128]{4,3,2,1,0:T(8,128)(2,1)S(1)}, bf16[1,9,3,32,128]{4,3,2,1,0:T(8,128)(2,1)}, u32[]{:S(2)}) copy-start(bf16[1,9,3,32,128]{4,3,2,1,0:T(8,128)(2,1)} %param.4) | copy-start | bytes 663556
  49.9 30.7 %all-to-all-start.1 = ((f32[32,1,129]{2,1,0:T(1,128)}), f32[32,1,129]{2,1,0:T(1,128)}, u32[]{:S(2)}, u32[]{:S(2)}) async-start(f32[32,1,129]{2,1,0:T(1,128)} %reshape.338), calls=%async_computation.1 | async-start | bytes 65536 | tf_op jit(solution)/shard_map/all_to_all | solution.py:33
  63.6 2.1 %copy-start.29 = (bf16[1,9,3,32,128]{4,3,2,1,0:T(8,128)(2,1)S(1)}, bf16[1,9,3,32,128]{4,3,2,1,0:T(8,128)(2,1)}, u32[]{:S(2)}) copy-start(bf16[1,9,3,32,128]{4,3,2,1,0:T(8,128)(2,1)} %slice.628) | copy-start | bytes 663556
  63.6 2.1 %copy-start.30 = (bf16[1,9,3,32,128]{4,3,2,1,0:T(8,128)(2,1)S(1)}, bf16[1,9,3,32,128]{4,3,2,1,0:T(8,128)(2,1)}, u32[]{:S(2)}) copy-start(bf16[1,9,3,32,128]{4,3,2,1,0:T(8,128)(2,1)} %get-tuple-element.4) | copy-start | bytes 663556
  65.7 1.3 copy-start.19
  65.8 1.3 copy-start.20
  65.8 1.3 copy-start.21
  65.8 1.3 copy-start.22
  65.8 1.3 copy-start.23
  65.8 1.4 copy-start.24
  68.6 1.3 copy-start.2
  69.9 1.3 copy-start.6
  71.2 1.3 copy-start.8
  72.4 1.3 copy-start.13
  72.4 1.3 copy-start.14
  72.4 1.3 copy-start.15
  72.4 1.3 copy-start.16
  72.4 1.3 copy-start.17
  72.5 1.4 copy-start.18
  74.1 1.3 copy-start.4
  75.3 1.3 copy-start.10
  75.3 1.3 copy-start.11
  75.3 1.3 copy-start.12
  80.6 57.1 %all-to-all-start = ((f32[32,108,128]{2,1,0:T(8,128)}), f32[32,108,128]{2,1,0:T(8,128)S(1)}, u32[]{:S(2)}, u32[]{:S(2)}) async-start(f32[32,108,128]{2,1,0:T(8,128)} %reshape.336), calls=%async_computation | async-start | bytes 3670016 | tf_op jit(solution)/shard_map/all_to_all | solution.py:33
  (6 other events, 5.4 us)
where the time goes:
time: 156 us
  waiting for transfers between devices  46 us (29%)
  starting transfers between devices  34.7 us (22%)
  matrix products  24 us (15%)
  local copies, waits for them, and re-layouts  20.5 us (13%)
  other arithmetic  14.2 us (9%)
  blocking collectives  13.3 us (9%)
  between operations  3.13 us (2%)
    all_to_all x2, waiting for transfers between devices, sent_and_summed(): lax.all_to_all(pieces, axis, split_axis=0, concat_axis=0, tiled=True)  46 us
    all_to_all x2, starting transfers between devices, sent_and_summed(): lax.all_to_all(pieces, axis, split_axis=0, concat_axis=0, tiled=True)  23.5 us
    all_to_all x1, blocking collectives, sent_to_all(): lax.all_to_all(jnp.broadcast_to(value[None], (count, *value.shape)), axis...  13.3 us
    dot_general x27, matrix products, conv_cells(): jnp.dot(joined, stacked[3 * tap_f + tap_w], preferred_element_type=jnp.fl...  12.6 us
    dot_general x9, matrix products, wgrad_cells(): lax.dot_general(left_all, right_all, (((0,), (0,)), ((), ())), preferred_...  11.4 us
    slice x6, local copies, waits for them, and re-layouts, conv_cells(): padded[:, off_frame:off_frame + frames, off_column:off_column + columns,...  7.25 us
    ppermute x2, starting transfers between devices, padded_2(): lax.ppermute(head, axis, [((i + 1) % count, i) for i in range(ends)])  7 us
    concatenate x22, other arithmetic, conv_cells(): joined = jnp.concatenate(pieces, axis=-1).reshape(-1, 3 * channels)  5.18 us
  transfers between devices with their start and end apart: 6, of which 1 were waited for; matrix products, arithmetic and copies ran while one was open for 21% of the time, Pallas kernels for 0%

commit v1 on v0

v1 whole, which is shorter than its diff:
```python
import jax
import jax.numpy as jnp
from jax import lax
from jax.experimental import pallas as pl
from jax.experimental.pallas import tpu as pltpu
from jax.sharding import PartitionSpec as P

r1_weight = 10.0
F32, BF16 = jnp.float32, jnp.bfloat16
C = 128
ROWS = 32
FR = 9
BLOCK = 112


def shifted_store(src, dst, frame, columns):
    for c in range(3):
        v = src[frame, 0:columns, 7 + c : 39 + c, :]
        dst[frame + 1, 0:columns, :, c * C : (c + 1) * C] = v.astype(BF16)


def zero_edges(src, dst, columns):
    src[:, :, 0:8, :] = jnp.zeros((FR, columns, 8, C), F32)
    src[:, :, 40:48, :] = jnp.zeros((FR, columns, 8, C), F32)
    dst[0] = jnp.zeros((columns, ROWS, 3 * C), BF16)
    dst[FR + 1] = jnp.zeros((columns, ROWS, 3 * C), BF16)


def conv(src, f0, frames, columns, weight):
    pieces = []
    for a in range(3):
        for b in range(3):
            v = src[f0 + a : f0 + a + frames, b : b + columns, :, :]
            pieces.append(v.reshape(frames * columns * ROWS, 3 * C))
    lhs = jnp.concatenate(pieces, axis=1)
    return jnp.dot(lhs, weight[...], preferred_element_type=F32)


def kernel(t_ref, x_ref, xp_ref, xb_ref, u_ref, up_ref, ub_ref, w_ref, wf_ref, bias_ref,
           keep_ref, send_ref, xf, x3, ue, gf, g3, ff, f3, bd, cv, gw):
    t = t_ref[0]
    s = lax.rem(t, 2)
    pcol = 6 - 6 * s
    bcol = 6 * s
    zero_edges(xf, x3, 9)
    zero_edges(gf, g3, 7)
    zero_edges(ff, f3, 5)
    xf[:, 3:6, 8:40, :] = x_ref[0].astype(F32)
    xf[:, pl.ds(pcol, 3), 8:40, :] = xp_ref[0].astype(F32)
    xf[:, pl.ds(bcol, 3), 8:40, :] = xb_ref[0].astype(F32)
    ue[:, 3:6] = u_ref[0]
    ue[:, pl.ds(pcol, 3)] = up_ref[0]
    ue[:, pl.ds(bcol, 3)] = ub_ref[0]
    for f in range(FR):
        shifted_store(xf, x3, f, 9)
    bias = bias_ref[...]
    for f0 in range(0, FR, 3):
        h = conv(x3, f0, 3, 7, w_ref) + bias
        sig = jax.nn.sigmoid(h).reshape(3, 7, ROWS, C)
        u = ue[f0 : f0 + 3, 1:8].astype(F32)
        gf[f0 : f0 + 3, :, 8:40, :] = u * (0.2 + 0.8 * sig)
        so = sig[:, 2:5]
        bd[f0 : f0 + 3] = u[:, 2:5] * (0.8 * so * (1.0 - so))
        for f in range(f0, f0 + 3):
            shifted_store(gf, g3, f, 7)
    left_in = jnp.where(t > 0, 1.0, 0.0)
    right_in = jnp.where(t < 31, 1.0, 0.0)
    squares = jnp.zeros((8, C), F32)
    for f0 in range(0, FR, 3):
        gx = conv(g3, f0, 3, 5, wf_ref).reshape(3, 5, ROWS, C)
        own = gx[:, 1:4]
        squares = squares + jnp.sum((own * own).reshape(36, 8, C), axis=0)
        ff[f0 : f0 + 3, 1:4, 8:40, :] = own
        ff[f0 : f0 + 3, 0:1, 8:40, :] = gx[:, 0:1] * left_in
        ff[f0 : f0 + 3, 4:5, 8:40, :] = gx[:, 4:5] * right_in
        for f in range(f0, f0 + 3):
            shifted_store(ff, f3, f, 5)
    bias_sum = jnp.zeros((8, C), F32)
    for f0 in range(0, FR, 3):
        bc = conv(f3, f0, 3, 3, w_ref).reshape(3, 3, ROWS, C)
        cu = (bc * bd[f0 : f0 + 3]).astype(BF16).astype(F32)
        bias_sum = bias_sum + jnp.sum(cu.reshape(36, 8, C), axis=0)
        cv[f0 : f0 + 3] = cu
    right = jnp.concatenate(
        [gf[:, 2:5, 8:40, :].reshape(FR * 96, C), cv[...].reshape(FR * 96, C)], axis=0
    )
    rt = right.T.astype(BF16)
    for a in range(3):
        cols = []
        for b in range(3):
            cols.append(
                jnp.concatenate(
                    [
                        f3[a : a + FR, b : b + 3].reshape(FR * 96, 3 * C),
                        x3[a : a + FR, 2 + b : 5 + b].reshape(FR * 96, 3 * C),
                    ],
                    axis=0,
                )
            )
        left = jnp.concatenate(cols, axis=1)
        g = jnp.dot(rt, left, preferred_element_type=F32)
        for k in range(9):
            gw[(9 * a + k) * C : (9 * a + k + 1) * C, :] = g[:, k * C : (k + 1) * C].T
    bias_row = jnp.sum(bias_sum, axis=0, keepdims=True)
    sq_row = jnp.sum(squares, axis=0, keepdims=True)
    stats = jnp.concatenate([bias_row, bias_row, sq_row, sq_row], axis=0)
    for core in range(2):

        @pl.when(s == core)
        def _():
            for j in range(32):
                ref = keep_ref if j % 2 == core else send_ref
                ref[j // 2, 0:108, :] = gw[108 * j : 108 * j + 108, :]
                ref[j // 2, 108:112, :] = stats


def compute(t, x, xp, xb, u, up, ub, w, wf, bias):
    vm = pl.BlockSpec(memory_space=pltpu.VMEM)
    return pl.pallas_call(
        kernel,
        in_specs=[pl.BlockSpec(memory_space=pltpu.SMEM)] + [vm] * 9,
        out_specs=[vm, vm],
        out_shape=[jax.ShapeDtypeStruct((16, BLOCK, C), F32)] * 2,
        scratch_shapes=[
            pltpu.VMEM((FR, 9, 48, C), F32),
            pltpu.VMEM((FR + 2, 9, ROWS, 3 * C), BF16),
            pltpu.VMEM((FR, 9, ROWS, C), BF16),
            pltpu.VMEM((FR, 7, 48, C), F32),
            pltpu.VMEM((FR + 2, 7, ROWS, 3 * C), BF16),
            pltpu.VMEM((FR, 5, 48, C), F32),
            pltpu.VMEM((FR + 2, 5, ROWS, 3 * C), BF16),
            pltpu.VMEM((FR, 3, ROWS, C), F32),
            pltpu.VMEM((FR, 3, ROWS, C), F32),
            pltpu.VMEM((27 * C, C), F32),
        ],
        compiler_params=pltpu.CompilerParams(vmem_limit_bytes=48 * 1024 * 1024),
        name="r1_section",
    )(t, x, xp, xb, u, up, ub, w, wf, bias)


def shards(clip_features, upstream, weight, conv_bias):
    tiles = 32
    factor = r1_weight / 221184
    w = weight.reshape(27 * C, C)
    wf = jnp.swapaxes(weight[::-1], 1, 2).reshape(27 * C, C)
    swap = [(i, i ^ 1) for i in range(tiles)]
    pairs = []
    for i in range(1, tiles - 1, 2):
        pairs += [(i, i + 1), (i + 1, i)]
    xb = lax.ppermute(clip_features, "tile", pairs)
    xp = lax.ppermute(clip_features, "tile", swap)
    up = lax.ppermute(upstream, "tile", swap)
    ub = lax.ppermute(upstream, "tile", pairs)
    t = lax.axis_index("tile").astype(jnp.int32).reshape(1)
    keep, send = compute(t, clip_features, xp, xb, upstream, up, ub, w, wf, conv_bias.reshape(1, C))
    both = keep + lax.ppermute(send, "tile", swap)
    row = lax.broadcasted_iota(jnp.int32, (1, BLOCK, 1), 1)
    low = (row == 109) | (row == 111)
    rounded = lax.reduce_precision(both, 8, 7)
    both = jnp.where(low, both - rounded, both).astype(BF16)
    groups = [[2 * i + c for i in range(16)] for c in range(2)]
    got = lax.all_to_all(both, "tile", 0, 0, axis_index_groups=groups, tiled=True)
    mine = jnp.sum(got.astype(F32), axis=0)
    everyone = lax.all_to_all(
        jnp.broadcast_to(mine[None], (8, BLOCK, C)), "clip", 0, 0, tiled=True
    )
    total = jnp.sum(everyone, axis=0)
    grad_bias = factor * (total[108] + total[109])
    penalty = 0.5 * factor * jnp.sum(total[110] + total[111])
    return factor * total[:108], grad_bias, penalty


def solution(mesh):
    in_specs = (P("clip", None, "tile", None, None), P("clip", None, "tile", None, None), P(), P())
    out_specs = (P("tile", None), P(), P())
    return jax.shard_map(shards, mesh=mesh, in_specs=in_specs, out_specs=out_specs, check_vma=False)
```

time: 156 us -> 70.9 us (0.45)
  waiting for transfers between devices: 46 us -> 3.41 us
  starting transfers between devices: 34.7 us -> 6.93 us
  blocking collectives: 13.3 us -> 40.2 us
  matrix products: 24 us -> 0 us
  local copies, waits for them, and re-layouts: 20.5 us -> 4.85 us
  other arithmetic: 14.2 us -> 2.04 us
  Pallas kernels: 0 us -> 10.7 us
    all_to_all x2 -> x0, waiting for transfers between devices: 46 us -> none  [sent_and_summed(): lax.all_to_all(pieces, axis, split_axis=0, concat_axis=0, tiled=True)]
    all_to_all x1 -> x2, blocking collectives: 13.3 us -> 40.2 us  [the longest x1 26.7 us: shards(): lax.all_to_all(both, 'tile', 0, 0, axis_index_groups=groups, tiled=True)]
    dot_general x36 -> x0, matrix products: 24 us -> none  [the longest x27 12.6 us: conv_cells(): jnp.dot(joined, stacked[3 * tap_f + tap_w], preferred_element_type=jnp.fl...]
    all_to_all x2 -> x0, starting transfers between devices: 23.5 us -> none  [sent_and_summed(): lax.all_to_all(pieces, axis, split_axis=0, concat_axis=0, tiled=True)]
    slice x14 -> x0, local copies, waits for them, and re-layouts: 13.6 us -> none  [the longest x6 7.25 us: conv_cells(): padded[:, off_frame:off_frame + frames, off_column:off_column + columns,...]
    pallas_call x0 -> x1, Pallas kernels: none -> 10.7 us  [compute(): pl.pallas_call(kernel, in_specs=[pl.BlockSpec(memory_space=pltpu.SMEM)] +...]
    concatenate x28 -> x0, other arithmetic: 8.63 us -> none  [the longest x22 5.18 us: conv_cells(): joined = jnp.concatenate(pieces, axis=-1).reshape(-1, 3 * channels)]
    ppermute x4 -> x5, starting transfers between devices: 11.3 us -> 6.93 us  [the longest x1 3.81 us: shards(): xb = lax.ppermute(clip_features, 'tile', pairs)]
  transfers between devices with their start and end apart: 6 -> 5, of which waited for: 1 -> 2; matrix products, arithmetic and copies ran while one was open for 21% -> 6% of each run, Pallas kernels for 0% -> 0%
where the time goes in v1:
time: 70.9 us; the launch traced here: 70.6 us
  blocking collectives  40.2 us (57%)
  Pallas kernels  10.7 us (15%)
  starting transfers between devices  6.93 us (10%)
  local copies, waits for them, and re-layouts  4.85 us (7%)
  waiting for transfers between devices  3.41 us (5%)
  between operations  2.5 us (4%)
  other arithmetic  2.04 us (3%)
    all_to_all x1, blocking collectives, shards(): lax.all_to_all(both, 'tile', 0, 0, axis_index_groups=groups, tiled=True)  26.7 us
    all_to_all x1, blocking collectives, shards(): lax.all_to_all(jnp.broadcast_to(mine[None], (8, BLOCK, C)), 'clip', 0, 0,...  13.5 us
    pallas_call x1, Pallas kernels, compute(): pl.pallas_call(kernel, in_specs=[pl.BlockSpec(memory_space=pltpu.SMEM)] +...  10.7 us
    transpose x2, local copies, waits for them, and re-layouts, shards(): wf = jnp.swapaxes(weight[::-1], 1, 2).reshape(27 * C, C)  4.17 us
    ppermute x1, starting transfers between devices, shards(): xb = lax.ppermute(clip_features, 'tile', pairs)  3.81 us
    ppermute x1, waiting for transfers between devices, shards(): both = keep + lax.ppermute(send, 'tile', swap)  2.09 us
    ppermute x1, starting transfers between devices, shards(): ub = lax.ppermute(upstream, 'tile', pairs)  1.91 us
  transfers between devices with their start and end apart: 5, of which 2 were waited for; matrix products, arithmetic and copies ran while one was open for 6% of the time, Pallas kernels for 0%

profile of v1, /device:TPU:32, one launch (start us, length us, event | category | flops | bytes accessed | tf_op | source)
XLA Modules:
  0.0 70.6 jit_solution(3108370881117330238)
XLA Ops:
  0.6 0.1 collective-permute-start
  0.7 3.8 %collective-permute-start.1 = (bf16[1,9,3,32,128]{4,3,2,1,0:T(8,128)(2,1)}, bf16[1,9,3,32,128]{4,3,2,1,0:T(8,128)(2,1)S(1)}, u32[]{:S(2)}, u32[]{:S(2)}) collective-permute-start(bf16[1,9,3,32,128]{4,3,2,1,0:T(8,128)(2,1)} %x_ref.1), channel_id=1, source_target_pairs={{1,2},{2,1},{3,4},{4,3},{5,6},{6,5},{7,8},{8,7},{9,10},{10,9},{11,... | collective-permute-start | bytes 663560 | tf_op jit(solution)/shard_map/ppermute | solution.py:150
  4.6 0.2 collective-permute-start.2
  4.8 1.9 %collective-permute-start.3 = (bf16[1,9,3,32,128]{4,3,2,1,0:T(8,128)(2,1)}, bf16[1,9,3,32,128]{4,3,2,1,0:T(8,128)(2,1)S(1)}, u32[]{:S(2)}, u32[]{:S(2)}) collective-permute-start(bf16[1,9,3,32,128]{4,3,2,1,0:T(8,128)(2,1)} %u_ref.1), channel_id=1, source_target_pairs={{1,2},{2,1},{3,4},{4,3},{5,6},{6,5},{7,8},{8,7},{9,10},{10,9},{11,... | collective-permute-start | bytes 663560 | tf_op jit(solution)/shard_map/ppermute | solution.py:153
  6.7 2.2 %reverse_bitcast_fusion = bf16[27,128,128]{1,2,0:T(8,128)(2,1)} fusion(bf16[27,128,128]{2,1,0:T(8,128)(2,1)} %param.6), kind=kLoop, calls=%fused_computation.3 | loop fusion | bytes 1769472 | tf_op jit(solution)/shard_map/transpose | solution.py:145
  8.9 0.0 copy-start
  8.9 0.0 copy-start.1
  8.9 0.0 copy-start.2
  8.9 2.0 %copy.8 = bf16[27,128,128]{2,1,0:T(8,128)(2,1)S(1)} copy(bf16[27,128,128]{1,2,0:T(8,128)(2,1)} %reverse_bitcast_fusion) | data formatting | bytes 1769472 | tf_op jit(solution)/shard_map/transpose | solution.py:145
  10.9 0.0 collective-permute-done.xp_ref
  10.9 0.0 collective-permute-done.1.xb_ref
  10.9 0.0 collective-permute-done.2.up_ref
  10.9 1.3 %collective-permute-done.3.ub_ref = bf16[1,9,3,32,128]{4,3,2,1,0:T(8,128)(2,1)S(1)} collective-permute-done((bf16[1,9,3,32,128]{4,3,2,1,0:T(8,128)(2,1)}, bf16[1,9,3,32,128]{4,3,2,1,0:T(8,128)(2,1)S(1)}, u32[]{:S(2)}, u32[]{:S(2)}) %collective-permute-start.3) | collective-permute-done | bytes 221216 | tf_op jit(solution)/shard_map/ppermute | solution.py:153
  12.2 0.0 copy-start.3
  12.2 0.0 copy-done
  12.2 0.0 copy-done.1
  12.2 0.0 copy-done.2
  12.2 0.6 copy-done.3
  12.9 10.7 %r1_section.1 = (f32[16,112,128]{2,1,0:T(8,128)S(1)}, f32[16,112,128]{2,1,0:T(8,128)S(1)}) custom-call(s32[1]{0:T(128)} %bitcast.t_ref, bf16[1,9,3,32,128]{4,3,2,1,0:T(8,128)(2,1)S(1)} %copy-done.1, bf16[1,9,3,32,128]{4,3,2,1,0:T(8,128)(2,1)S(1)} %collective-permute-done.xp_ref, bf16[1,9,3,32,128]{4,3,2,1,0:T(8,128)(2,1)S(1)} %collective-permute-done.1.xb_ref, ...), custom_call_target="tpu_custom_call" | custom-call | tf_op jit(solution)/shard_map/r1_section/pallas_call | solution.py:119
  23.6 0.9 %collective-permute-start.4 = (f32[16,112,128]{2,1,0:T(8,128)S(1)}, f32[16,112,128]{2,1,0:T(8,128)S(1)}, u32[]{:S(2)}, u32[]{:S(2)}) collective-permute-start(f32[16,112,128]{2,1,0:T(8,128)S(1)} %get-tuple-element.6), channel_id=1, source_target_pairs={{0,1},{1,0},{2,3},{3,2},{4,5},{5,4},{6,7},{7,6},{8,9},{9,8},{10,11... | collective-permute-start | bytes 2752520 | tf_op jit(solution)/shard_map/ppermute | solution.py:156
  24.5 2.1 %collective-permute-done.4 = f32[16,112,128]{2,1,0:T(8,128)S(1)} collective-permute-done((f32[16,112,128]{2,1,0:T(8,128)S(1)}, f32[16,112,128]{2,1,0:T(8,128)S(1)}, u32[]{:S(2)}, u32[]{:S(2)}) %collective-permute-start.4) | collective-permute-done | bytes 917536 | tf_op jit(solution)/shard_map/ppermute | solution.py:156
  26.6 0.2 fusion
  26.8 26.7 %all_to_all.10 = bf16[16,112,128]{2,1,0:T(8,128)(2,1)S(1)} all-to-all(bf16[16,112,128]{2,1,0:T(8,128)(2,1)S(1)} %fusion), channel_id=1, replica_groups={{0,2,4,6,8,10,12,14,16,18,20,22,24,26,28,30},{1,3,5,7,9,11,13,15,17,19,..., dimensions={0} | all-to-all | bytes 917504 | tf_op jit(solution)/shard_map/all_to_all | solution.py:162
  53.4 0.1 convert_reduce_fusion
  53.5 13.5 %all_to_all.11 = f32[8,112,128]{2,1,0:T(8,128)S(1)} all-to-all(f32[8,112,128]{2,1,0:T(8,128)S(1)} %broadcast_in_dim.15), channel_id=1, replica_groups=mesh['clip'=8,'tile'=32] {'clip'}, dimensions={0} | all-to-all | bytes 917504 | tf_op jit(solution)/shard_map/all_to_all | solution.py:164
  67.1 1.1 %fusion.1 = (f32[]{:T(128)}, f32[128]{0:T(128)}) fusion(f32[112,128]{1,0:T(8,128)S(1)} %reduce_sum.28), kind=kLoop, calls=%fused_computation.7 | loop fusion | flops 511 | bytes 2564 | tf_op jit(solution)/shard_map/reduce_sum | solution.py:169
  68.2 0.6 slice_multiply_fusion
  (3 shorter events, 0.1 us)
Async XLA Ops:
  0.6 10.3 %collective-permute-start = (bf16[1,9,3,32,128]{4,3,2,1,0:T(8,128)(2,1)}, bf16[1,9,3,32,128]{4,3,2,1,0:T(8,128)(2,1)S(1)}, u32[]{:S(2)}, u32[]{:S(2)}) collective-permute-start(bf16[1,9,3,32,128]{4,3,2,1,0:T(8,128)(2,1)} %x_ref.1), channel_id=1, source_target_pairs={{0,1},{1,0},{2,3},{3,2},{4,5},{5,4},{6,7},{7,6},{8,9},{9,8},{10,11... | collective-permute-start | bytes 663560 | tf_op jit(solution)/shard_map/ppermute | solution.py:151
  0.7 10.2 %collective-permute-start.1 = (bf16[1,9,3,32,128]{4,3,2,1,0:T(8,128)(2,1)}, bf16[1,9,3,32,128]{4,3,2,1,0:T(8,128)(2,1)S(1)}, u32[]{:S(2)}, u32[]{:S(2)}) collective-permute-start(bf16[1,9,3,32,128]{4,3,2,1,0:T(8,128)(2,1)} %x_ref.1), channel_id=1, source_target_pairs={{1,2},{2,1},{3,4},{4,3},{5,6},{6,5},{7,8},{8,7},{9,10},{10,9},{11,... | collective-permute-start | bytes 663560 | tf_op jit(solution)/shard_map/ppermute | solution.py:150
  4.6 6.3 %collective-permute-start.2 = (bf16[1,9,3,32,128]{4,3,2,1,0:T(8,128)(2,1)}, bf16[1,9,3,32,128]{4,3,2,1,0:T(8,128)(2,1)S(1)}, u32[]{:S(2)}, u32[]{:S(2)}) collective-permute-start(bf16[1,9,3,32,128]{4,3,2,1,0:T(8,128)(2,1)} %u_ref.1), channel_id=1, source_target_pairs={{0,1},{1,0},{2,3},{3,2},{4,5},{5,4},{6,7},{7,6},{8,9},{9,8},{10,11... | collective-permute-start | bytes 663560 | tf_op jit(solution)/shard_map/ppermute | solution.py:152
  4.8 7.5 %collective-permute-start.3 = (bf16[1,9,3,32,128]{4,3,2,1,0:T(8,128)(2,1)}, bf16[1,9,3,32,128]{4,3,2,1,0:T(8,128)(2,1)S(1)}, u32[]{:S(2)}, u32[]{:S(2)}) collective-permute-start(bf16[1,9,3,32,128]{4,3,2,1,0:T(8,128)(2,1)} %u_ref.1), channel_id=1, source_target_pairs={{1,2},{2,1},{3,4},{4,3},{5,6},{6,5},{7,8},{8,7},{9,10},{10,9},{11,... | collective-permute-start | bytes 663560 | tf_op jit(solution)/shard_map/ppermute | solution.py:153
  8.9 3.4 %copy-start = (bf16[27,128,128]{2,1,0:T(8,128)(2,1)S(1)}, bf16[27,128,128]{2,1,0:T(8,128)(2,1)}, u32[]{:S(2)}) copy-start(bf16[27,128,128]{2,1,0:T(8,128)(2,1)} %param.6) | copy-start | bytes 2654212
  8.9 3.4 %copy-start.1 = (bf16[1,9,3,32,128]{4,3,2,1,0:T(8,128)(2,1)S(1)}, bf16[1,9,3,32,128]{4,3,2,1,0:T(8,128)(2,1)}, u32[]{:S(2)}) copy-start(bf16[1,9,3,32,128]{4,3,2,1,0:T(8,128)(2,1)} %x_ref.1) | copy-start | bytes 663556
  8.9 3.4 %copy-start.2 = (bf16[1,9,3,32,128]{4,3,2,1,0:T(8,128)(2,1)S(1)}, bf16[1,9,3,32,128]{4,3,2,1,0:T(8,128)(2,1)}, u32[]{:S(2)}) copy-start(bf16[1,9,3,32,128]{4,3,2,1,0:T(8,128)(2,1)} %u_ref.1) | copy-start | bytes 663556
  12.2 0.7 copy-start.3
  23.6 3.0 %collective-permute-start.4 = (f32[16,112,128]{2,1,0:T(8,128)S(1)}, f32[16,112,128]{2,1,0:T(8,128)S(1)}, u32[]{:S(2)}, u32[]{:S(2)}) collective-permute-start(f32[16,112,128]{2,1,0:T(8,128)S(1)} %get-tuple-element.6), channel_id=1, source_target_pairs={{0,1},{1,0},{2,3},{3,2},{4,5},{5,4},{6,7},{7,6},{8,9},{9,8},{10,11... | collective-permute-start | bytes 2752520 | tf_op jit(solution)/shard_map/ppermute | solution.py:156

commit v2 on v1

v2 whole, which is shorter than its diff:
```python
import jax
import jax.numpy as jnp
from jax import lax
from jax.experimental import pallas as pl
from jax.experimental.pallas import tpu as pltpu
from jax.sharding import PartitionSpec as P

r1_weight = 10.0
factor = r1_weight / 221184
F32, BF16 = jnp.float32, jnp.bfloat16
C = 128
ROWS = 32
FR = 9
TILES = 32
BLOCK = 112


def place(frame):
    return (frame + 1) // 2, (frame + 1) % 2


def spread_rows(src, dst, frames, src_col, dst_col, columns):
    for f in frames:
        p, r = place(f)
        for c in range(3):
            v = src[f, pl.ds(src_col, columns), 7 + c : 39 + c, :]
            dst[p, r, pl.ds(dst_col, columns), :, c * C : (c + 1) * C] = v.astype(BF16)


def zero_rows(src, columns):
    src[:, :, 0:8, :] = jnp.zeros((FR, columns, 8, C), F32)
    src[:, :, 40:48, :] = jnp.zeros((FR, columns, 8, C), F32)


def zero_frames(dst, columns):
    for f in (-1, 9, 10):
        p, r = place(f)
        dst[p, r] = jnp.zeros((columns, ROWS, 3 * C), BF16)


def conv(src, p0, pairs, col, columns, weight):
    pieces = []
    for a in range(4):
        for b in range(3):
            p = p0 + a // 2
            v = src[p : p + pairs, a % 2, pl.ds(col + b, columns), :, :]
            pieces.append(v.reshape(pairs * columns * ROWS, 3 * C))
    lhs = jnp.concatenate(pieces, axis=1)
    out = jnp.dot(lhs, weight[...], preferred_element_type=F32)
    out = out.reshape(pairs, columns, ROWS, 2 * C)
    return [
        (2 * (p0 + i) + r, out[i, :, :, r * C : (r + 1) * C])
        for i in range(pairs)
        for r in range(2)
        if 2 * (p0 + i) + r < FR
    ]


GROUPS = ((0, 3), (3, 2))


def hidden_part(x3, ue, gf, bd, g3, weight, bias, col, columns):
    for p0, pairs in GROUPS:
        for f, out in conv(x3, p0, pairs, col, columns, weight):
            sig = jax.nn.sigmoid(out + bias)
            u = ue[f, pl.ds(col + 1, columns)].astype(F32)
            gf[f, 0:columns, 8:40, :] = u * (0.2 + 0.8 * sig)
            bd[f, pl.ds(col, columns)] = u * (0.8 * sig * (1.0 - sig))
            spread_rows(gf, g3, (f,), 0, col, columns)


def grad_part(g3, ff, f3, weight, col, columns, masks, shares):
    squares = [jnp.zeros((8, C), F32) for _ in range(columns)]
    for p0, pairs in GROUPS:
        for f, gx in conv(g3, p0, pairs, col, columns, weight):
            for q in range(columns):
                v = gx[q]
                if masks[q] is not None:
                    v = v * masks[q]
                ff[f, q, 8:40, :] = v
                squares[q] = squares[q] + jnp.sum((v * v).reshape(4, 8, C), axis=0)
            spread_rows(ff, f3, (f,), 0, col, columns)
    return sum(v * share for v, share in zip(squares, shares))


def gather_kernel(t_ref, x_ref, u_ref, own_ref, edge_ref, sems):
    s = lax.rem(t_ref[0], 2)
    copies = (
        pltpu.make_async_copy(x_ref.at[0], edge_ref.at[:, pl.ds(0, 3)], sems.at[0]),
        pltpu.make_async_copy(u_ref.at[0, :, pl.ds(s, 2)], edge_ref.at[:, pl.ds(3, 2)], sems.at[1]),
        pltpu.make_async_copy(x_ref.at[0], own_ref.at[0], sems.at[2]),
        pltpu.make_async_copy(u_ref.at[0], own_ref.at[1], sems.at[3]),
    )
    for copy in copies:
        copy.start()
    for copy in copies:
        copy.wait()


def near_kernel(t_ref, o_ref, p_ref, w_ref, bias_ref,
                x3, g3, f3, bd, wp, wfp, bias, sq, xf, ue, gf, ff, sems):
    s = lax.rem(t_ref[0], 2)
    pcol = 6 - 6 * s
    copies = (
        pltpu.make_async_copy(w_ref, wp.at[0 : 27 * C, 0:C], sems.at[0]),
        pltpu.make_async_copy(w_ref, wp.at[9 * C : 36 * C, C : 2 * C], sems.at[1]),
        pltpu.make_async_copy(bias_ref, bias, sems.at[2]),
    )
    for copy in copies:
        copy.start()
    for m in (wp, wfp):
        m[27 * C : 36 * C, 0:C] = jnp.zeros((9 * C, C), BF16)
        m[0 : 9 * C, C : 2 * C] = jnp.zeros((9 * C, C), BF16)
    zero_rows(xf, 6)
    zero_rows(gf, 4)
    zero_rows(ff, 2)
    zero_frames(x3, 9)
    zero_frames(g3, 7)
    zero_frames(f3, 5)
    xf[:, 0:3, 8:40, :] = o_ref[0].astype(F32)
    xf[:, 3:6, 8:40, :] = p_ref[0].astype(F32)
    ue[:, 3:6] = o_ref[1]
    ue[:, pl.ds(pcol, 3)] = p_ref[1]
    spread_rows(xf, x3, range(FR), 0, 3, 3)
    spread_rows(xf, x3, range(FR), 3, pcol, 3)
    for copy in copies:
        copy.wait()
    for k in range(27):
        tap = wp[(26 - k) * C : (27 - k) * C, 0:C].astype(F32).T.astype(BF16)
        wfp[k * C : (k + 1) * C, 0:C] = tap
        wfp[(k + 9) * C : (k + 10) * C, C : 2 * C] = tap
    hidden_part(x3, ue, gf, bd, g3, wp, bias[...], 3 - 3 * s, 4)
    odd = s.astype(F32)
    sq[...] = grad_part(g3, ff, f3, wfp, 3 - 3 * s, 2, (None, None), (1.0 - odd, odd))


def far_kernel(t_ref, o_ref, b_ref, wp, wfp, bias_ref, sq_ref,
               x3_in, g3_in, f3_in, bd_in, keep_ref, send_ref, x3, g3, f3, bd,
               xf, ue, gf, ff, cv, gw):
    t = t_ref[0]
    s = lax.rem(t, 2)
    bcol = 6 * s
    zero_rows(xf, 3)
    zero_rows(gf, 3)
    zero_rows(ff, 3)
    xf[:, :, 8:40, :] = b_ref[:, 0:3].astype(F32)
    ue[:, 3:6] = o_ref[1]
    ue[:, pl.ds(1 + 5 * s, 2)] = b_ref[:, 3:5]
    spread_rows(xf, x3, range(FR), 0, bcol, 3)
    hidden_part(x3, ue, gf, bd, g3, wp, bias_ref[...], 4 * s, 3)
    odd = s.astype(F32)
    left_in = jnp.where(t == 0, 0.0, 1.0)
    right_in = jnp.where(t == TILES - 1, 0.0, 1.0)
    squares = sq_ref[...] + grad_part(
        g3, ff, f3, wfp, 2 * s, 3, (left_in, None, right_in), (odd, 1.0, 1.0 - odd)
    )
    bias_sum = jnp.zeros((8, C), F32)
    for p0, pairs in GROUPS:
        for f, bc in conv(f3, p0, pairs, 0, 3, wp):
            cu = (bc * bd[f, 2:5]).astype(BF16).astype(F32)
            bias_sum = bias_sum + jnp.sum(cu.reshape(12, 8, C), axis=0)
            cv[f] = cu
    own = [g3[(*place(f), slice(2, 5), slice(None), slice(C, 2 * C))] for f in range(FR)]
    own = jnp.concatenate([v.astype(F32).reshape(96, C) for v in own], axis=0)
    right = jnp.concatenate([own, cv[...].reshape(FR * 96, C)], axis=0)
    rt = right.T.astype(BF16)
    for a in range(3):
        cols = []
        for b in range(3):
            taps = [f3[(*place(f + a - 1), slice(b, b + 3))] for f in range(FR)]
            taps += [x3[(*place(f + a - 1), slice(2 + b, 5 + b))] for f in range(FR)]
            cols.append(jnp.concatenate([v.reshape(96, 3 * C) for v in taps], axis=0))
        left = jnp.concatenate(cols, axis=1)
        g = jnp.dot(rt, left, preferred_element_type=F32)
        for k in range(9):
            gw[(9 * a + k) * C : (9 * a + k + 1) * C, :] = g[:, k * C : (k + 1) * C].T
    bias_row = jnp.sum(bias_sum, axis=0, keepdims=True)
    sq_row = jnp.sum(squares, axis=0, keepdims=True)
    stats = jnp.concatenate([bias_row, bias_row, sq_row, sq_row], axis=0)
    for core in range(2):

        @pl.when(s == core)
        def _():
            for j in range(TILES):
                ref = keep_ref if j % 2 == core else send_ref
                ref[j // 2, 0:108, :] = gw[108 * j : 108 * j + 108, :]
                ref[j // 2, 108:112, :] = stats


def high_and_low(total):
    high = total.astype(BF16).astype(F32)
    return high, total - high


def middle_kernel(got_ref, out_ref):
    total = jnp.sum(got_ref[...].astype(F32), axis=0)
    bias = high_and_low(total[108:109] + total[109:110])
    squares = high_and_low(total[110:111] + total[111:112])
    full = jnp.concatenate([total[0:108], *bias, *squares], axis=0).astype(BF16)
    for i in range(8):
        out_ref[i] = full


def last_kernel(got_ref, grad_ref, bias_ref, penalty_ref):
    total = jnp.sum(got_ref[...].astype(F32), axis=0)
    grad_ref[...] = factor * total[0:108]
    bias_ref[...] = factor * (total[108:109] + total[109:110])
    square = jnp.sum(total[110:111] + total[111:112], axis=1, keepdims=True)
    penalty_ref[...] = 0.5 * factor * square


VM = pl.BlockSpec(memory_space=pltpu.VMEM)
SM = pl.BlockSpec(memory_space=pltpu.SMEM)
HB = pl.BlockSpec(memory_space=pltpu.HBM)


def params(mib):
    return pltpu.CompilerParams(vmem_limit_bytes=mib * 1024 * 1024)


def shape(dtype, *dims):
    return jax.ShapeDtypeStruct(dims, dtype)


def gather(t, x, u):
    return pl.pallas_call(
        gather_kernel,
        in_specs=[SM, HB, HB],
        out_specs=[VM] * 2,
        out_shape=[shape(BF16, 2, FR, 3, ROWS, C), shape(BF16, FR, 5, ROWS, C)],
        scratch_shapes=[pltpu.SemaphoreType.DMA((4,))],
        compiler_params=params(4),
        name="gather_own",
    )(t, x, u)


def near(t, own, p, w, bias):
    return pl.pallas_call(
        near_kernel,
        in_specs=[SM, VM, VM, HB, HB],
        out_specs=[VM] * 8,
        out_shape=[
            shape(BF16, 6, 2, 9, ROWS, 3 * C),
            shape(BF16, 6, 2, 7, ROWS, 3 * C),
            shape(BF16, 6, 2, 5, ROWS, 3 * C),
            shape(F32, FR, 7, ROWS, C),
            shape(BF16, 36 * C, 2 * C),
            shape(BF16, 36 * C, 2 * C),
            shape(F32, 1, C),
            shape(F32, 8, C),
        ],
        scratch_shapes=[
            pltpu.VMEM((FR, 6, 48, C), F32),
            pltpu.VMEM((FR, 9, ROWS, C), BF16),
            pltpu.VMEM((FR, 4, 48, C), F32),
            pltpu.VMEM((FR, 2, 48, C), F32),
            pltpu.SemaphoreType.DMA((3,)),
        ],
        compiler_params=params(24),
        cost_estimate=pl.CostEstimate(flops=4_000_000_000, bytes_accessed=8_000_000, transcendentals=0),
        name="near_columns",
    )(t, own, p, w, bias)


def far(t, own, b, wp, wfp, bias, sq, x3, g3, f3, bd):
    return pl.pallas_call(
        far_kernel,
        in_specs=[SM] + [VM] * 10,
        out_specs=[VM] * 6,
        out_shape=[shape(F32, 16, BLOCK, C)] * 2
        + [shape(v.dtype, *v.shape) for v in (x3, g3, f3, bd)],
        scratch_shapes=[
            pltpu.VMEM((FR, 3, 48, C), F32),
            pltpu.VMEM((FR, 9, ROWS, C), BF16),
            pltpu.VMEM((FR, 3, 48, C), F32),
            pltpu.VMEM((FR, 3, 48, C), F32),
            pltpu.VMEM((FR, 3, ROWS, C), F32),
            pltpu.VMEM((27 * C, C), F32),
        ],
        input_output_aliases={7: 2, 8: 3, 9: 4, 10: 5},
        compiler_params=params(24),
        cost_estimate=pl.CostEstimate(flops=6_000_000_000, bytes_accessed=8_000_000, transcendentals=0),
        name="far_columns",
    )(t, own, b, wp, wfp, bias, sq, x3, g3, f3, bd)[:2]


def shards(clip_features, upstream, weight, conv_bias):
    w = weight.reshape(27 * C, C)
    bias = conv_bias.reshape(1, C)
    swap = [(i, i ^ 1) for i in range(TILES)]
    pairs = []
    for i in range(1, TILES - 1, 2):
        pairs += [(i, i + 1), (i + 1, i)]
    t = lax.axis_index("tile").astype(jnp.int32).reshape(1)
    in_hbm = lambda v: pltpu.with_memory_space_constraint(v, pltpu.HBM)
    own, edge = gather(t, in_hbm(clip_features), in_hbm(upstream))
    other = lax.ppermute(edge, "tile", pairs)
    partner = lax.ppermute(own, "tile", swap)
    x3, g3, f3, bd, wp, wfp, bias, sq = near(t, own, partner, in_hbm(w), in_hbm(bias))
    keep, send = far(t, own, other, wp, wfp, bias, sq, x3, g3, f3, bd)
    total = keep + lax.ppermute(send, "tile", swap)
    row = lax.broadcasted_iota(jnp.int32, (1, BLOCK, 1), 1)
    low = (row == 109) | (row == 111)
    rounded = lax.reduce_precision(total, 8, 7)
    total = jnp.where(low, total - rounded, total).astype(BF16)
    groups = [[2 * i + c for i in range(16)] for c in range(2)]
    got = lax.all_to_all(total, "tile", 0, 0, axis_index_groups=groups, tiled=True)
    mine = pl.pallas_call(
        middle_kernel,
        in_specs=[VM],
        out_specs=VM,
        out_shape=jax.ShapeDtypeStruct((8, BLOCK, C), BF16),
        compiler_params=params(4),
        name="middle_sum",
    )(got)
    everyone = lax.all_to_all(mine, "clip", 0, 0, tiled=True)
    grad, grad_bias, penalty = pl.pallas_call(
        last_kernel,
        in_specs=[VM],
        out_specs=[VM] * 3,
        out_shape=[
            jax.ShapeDtypeStruct((108, C), F32),
            jax.ShapeDtypeStruct((1, C), F32),
            jax.ShapeDtypeStruct((1, 1), F32),
        ],
        compiler_params=params(4),
        name="last_sum",
    )(everyone)
    return grad, grad_bias.reshape(C), penalty.reshape(())


def solution(mesh):
    in_specs = (P("clip", None, "tile", None, None), P("clip", None, "tile", None, None), P(), P())
    out_specs = (P("tile", None), P(), P())
    return jax.shard_map(shards, mesh=mesh, in_specs=in_specs, out_specs=out_specs, check_vma=False)
```

time: 70.9 us -> 60.7 us (0.86)
  local copies, waits for them, and re-layouts: 4.85 us -> 0 us
  Pallas kernels: 10.7 us -> 14.1 us
  starting transfers between devices: 6.93 us -> 4.39 us
  other arithmetic: 2.04 us -> 0.21 us
  between operations: 2.5 us -> 0.69 us
  blocking collectives: 40.2 us -> 38.6 us
  waiting for transfers between devices: 3.41 us -> 2.48 us
    transpose x2 -> x0, local copies, waits for them, and re-layouts: 4.17 us -> none  [shards(): wf = jnp.swapaxes(weight[::-1], 1, 2).reshape(27 * C, C)]
    pallas_call x1 -> x5, Pallas kernels: 10.7 us -> 14.1 us  [the longest x1 7.3 us: far(): pl.pallas_call(far_kernel, in_specs=[SM] + [VM] * 10, out_specs=[VM] * 6,...]
    ppermute x5 -> x3, starting transfers between devices: 6.93 us -> 4.39 us  [the longest x1 3.81 us: shards(): other = lax.ppermute(edge, 'tile', pairs)]
    all_to_all x2, blocking collectives: 40.2 us -> 38.6 us  [the longest x1 27.2 us: shards(): lax.all_to_all(total, 'tile', 0, 0, axis_index_groups=groups, tiled=True)]
    reduce_sum x3 -> x0, other arithmetic: 1.21 us -> none  [the longest x1 1.12 us: shards(): penalty = 0.5 * factor * jnp.sum(total[110] + total[111])]
    ppermute x5 -> x3, waiting for transfers between devices: 3.41 us -> 2.48 us  [the longest x1 2.09 us: shards(): total = keep + lax.ppermute(send, 'tile', swap)]
  transfers between devices with their start and end apart: 5 -> 3, of which waited for: 2 -> 2; matrix products, arithmetic and copies ran while one was open for 6% -> 0% of each run, Pallas kernels for 0% -> 8%
where the time goes in v2:
time: 60.7 us; the launch traced here: 60.5 us
  blocking collectives  38.6 us (64%)
  Pallas kernels  14.1 us (23%)
  starting transfers between devices  4.39 us (7%)
  waiting for transfers between devices  2.48 us (4%)
  between operations  0.69 us (1%)
    all_to_all x1, blocking collectives, shards(): lax.all_to_all(total, 'tile', 0, 0, axis_index_groups=groups, tiled=True)  27.2 us
    all_to_all x1, blocking collectives, shards(): everyone = lax.all_to_all(mine, 'clip', 0, 0, tiled=True)  11.4 us
    pallas_call x1, Pallas kernels, far(): pl.pallas_call(far_kernel, in_specs=[SM] + [VM] * 10, out_specs=[VM] * 6,...  7.3 us
    pallas_call x1, Pallas kernels, near(): pl.pallas_call(near_kernel, in_specs=[SM, VM, VM, HB, HB], out_specs=[VM]...  4.78 us
    ppermute x1, starting transfers between devices, shards(): other = lax.ppermute(edge, 'tile', pairs)  3.81 us
    ppermute x1, waiting for transfers between devices, shards(): total = keep + lax.ppermute(send, 'tile', swap)  2.09 us
    pallas_call x1, Pallas kernels, gather(): pl.pallas_call(gather_kernel, in_specs=[SM, HB, HB], out_specs=[VM] * 2,...  1.27 us
  transfers between devices with their start and end apart: 3, of which 2 were waited for; matrix products, arithmetic and copies ran while one was open for 0% of the time, Pallas kernels for 8%

profile of v2, /device:TPU:32, one launch (start us, length us, event | category | flops | bytes accessed | tf_op | source)
XLA Modules:
  0.0 60.5 jit_solution(6690254617826698826)
XLA Ops:
  0.6 1.3 %gather_own.1 = (bf16[2,9,3,32,128]{4,3,2,1,0:T(8,128)(2,1)S(1)}, bf16[9,5,32,128]{3,2,1,0:T(8,128)(2,1)S(1)}) custom-call(s32[1]{0:T(128)} %bitcast.t_ref, bf16[1,9,3,32,128]{4,3,2,1,0:T(8,128)(2,1)} %x_ref.1, bf16[1,9,3,32,128]{4,3,2,1,0:T(8,128)(2,1)} %u_ref.1), custom_call_target="tpu_custom_call" | custom-call | tf_op jit(solution)/shard_map/gather_own/pallas_call | solution.py:226
  1.9 0.1 collective-permute-start.1
  2.0 3.8 %collective-permute-start = (bf16[9,5,32,128]{3,2,1,0:T(8,128)(2,1)S(1)}, bf16[9,5,32,128]{3,2,1,0:T(8,128)(2,1)S(1)}, u32[]{:S(2)}, u32[]{:S(2)}) collective-permute-start(bf16[9,5,32,128]{3,2,1,0:T(8,128)(2,1)S(1)} %get-tuple-element.19), channel_id=1, source_target_pairs={{1,2},{2,1},{3,4},{4,3},{5,6},{6,5},{7,8},{8,7},{9,10},{10,9},{11,... | collective-permute-start | bytes 1105928 | tf_op jit(solution)/shard_map/ppermute | solution.py:297
  5.8 0.0 collective-permute-done.1.p_ref
  5.8 4.8 %near_columns.1 = (bf16[6,2,9,32,384]{4,3,2,1,0:T(8,128)(2,1)S(1)}, bf16[6,2,7,32,384]{4,3,2,1,0:T(8,128)(2,1)S(1)}, bf16[6,2,5,32,384]{4,3,2,1,0:T(8,128)(2,1)S...) custom-call(s32[1]{0:T(128)} %bitcast.t_ref, ...), custom_call_target="tpu_custom_call" | custom-call | flops 4000000000 | bytes 8000000 | tf_op jit(solution)/shard_map/near_columns/pallas_call | solution.py:238
  10.6 0.4 collective-permute-done.b_ref
  11.0 7.3 %far_columns.1 = (f32[16,112,128]{2,1,0:T(8,128)S(1)}, f32[16,112,128]{2,1,0:T(8,128)S(1)}, bf16[6,2,9,32,384]{4,3,2,1,0:T(8,128)(2,1)S(1)}, bf16[6,2,7,32,384]{...) custom-call(s32[1]{0:T(128)} %bitcast.t_ref, ...), custom_call_target="tpu_custom_call", output_to_operand_aliasing={{2}: (7, {}), {3}: (8, {}), {4}: (9, {}), {5}: (10, {})} | custom-call | flops 6000000000 | bytes 8000000 | tf_op jit(solution)/shard_map/far_columns/pallas_call | solution.py:266
  18.3 0.5 collective-permute-start.2
  18.8 2.1 %collective-permute-done.2 = f32[16,112,128]{2,1,0:T(8,128)S(1)} collective-permute-done((f32[16,112,128]{2,1,0:T(8,128)S(1)}, f32[16,112,128]{2,1,0:T(8,128)S(1)}, u32[]{:S(2)}, u32[]{:S(2)}) %collective-permute-start.2) | collective-permute-done | bytes 917536 | tf_op jit(solution)/shard_map/ppermute | solution.py:301
  20.9 0.2 fusion
  21.1 27.2 %all_to_all.10.got_ref = bf16[16,112,128]{2,1,0:T(8,128)(2,1)S(1)} all-to-all(bf16[16,112,128]{2,1,0:T(8,128)(2,1)S(1)} %fusion), channel_id=1, replica_groups={{0,2,4,6,8,10,12,14,16,18,20,22,24,26,28,30},{1,3,5,7,9,11,13,15,17,19,..., dimensions={0} | all-to-all | bytes 917504 | tf_op jit(solution)/shard_map/all_to_all | solution.py:307
  48.3 0.1 middle_sum.1
  48.4 11.4 %all_to_all.11.got_ref = bf16[8,112,128]{2,1,0:T(8,128)(2,1)S(1)} all-to-all(bf16[8,112,128]{2,1,0:T(8,128)(2,1)S(1)} %middle_sum.1), channel_id=1, replica_groups=mesh['clip'=8,'tile'=32] {'clip'}, dimensions={0} | all-to-all | bytes 458752 | tf_op jit(solution)/shard_map/all_to_all | solution.py:316
  59.8 0.7 %last_sum.1 = (f32[108,128]{1,0:T(8,128)}, f32[1,128]{1,0:T(1,128)}, f32[1,1]{1,0:T(1,128)}) custom-call(bf16[8,112,128]{2,1,0:T(8,128)(2,1)S(1)} %all_to_all.11.got_ref), custom_call_target="tpu_custom_call" | custom-call | tf_op jit(solution)/shard_map/last_sum/pallas_call | solution.py:317
  (1 shorter events, 0.0 us)
Async XLA Ops:
  1.9 3.9 %collective-permute-start.1 = (bf16[2,9,3,32,128]{4,3,2,1,0:T(8,128)(2,1)S(1)}, bf16[2,9,3,32,128]{4,3,2,1,0:T(8,128)(2,1)S(1)}, u32[]{:S(2)}, u32[]{:S(2)}) collective-permute-start(bf16[2,9,3,32,128]{4,3,2,1,0:T(8,128)(2,1)S(1)} %get-tuple-element.18.o_ref), channel_id=1, source_target_pairs={{0,1},{1,0},{2,3},{3,2},{4,5},{5,4},{6,7},{7,6},{8,9},{9,8},{10,11... | collective-permute-start | bytes 1327112 | tf_op jit(solution)/shard_map/ppermute | solution.py:298
  2.0 9.0 %collective-permute-start = (bf16[9,5,32,128]{3,2,1,0:T(8,128)(2,1)S(1)}, bf16[9,5,32,128]{3,2,1,0:T(8,128)(2,1)S(1)}, u32[]{:S(2)}, u32[]{:S(2)}) collective-permute-start(bf16[9,5,32,128]{3,2,1,0:T(8,128)(2,1)S(1)} %get-tuple-element.19), channel_id=1, source_target_pairs={{1,2},{2,1},{3,4},{4,3},{5,6},{6,5},{7,8},{8,7},{9,10},{10,9},{11,... | collective-permute-start | bytes 1105928 | tf_op jit(solution)/shard_map/ppermute | solution.py:297
  18.3 2.6 %collective-permute-start.2 = (f32[16,112,128]{2,1,0:T(8,128)S(1)}, f32[16,112,128]{2,1,0:T(8,128)S(1)}, u32[]{:S(2)}, u32[]{:S(2)}) collective-permute-start(f32[16,112,128]{2,1,0:T(8,128)S(1)} %get-tuple-element.29), channel_id=1, source_target_pairs={{0,1},{1,0},{2,3},{3,2},{4,5},{5,4},{6,7},{7,6},{8,9},{9,8},{10,11... | collective-permute-start | bytes 2752520 | tf_op jit(solution)/shard_map/ppermute | solution.py:301

commit v3 on v2

--- a/solution.py
+++ b/solution.py
@@ -56,7 +56,7 @@
     ]
 
 
-GROUPS = ((0, 3), (3, 2))
+GROUPS = ((0, 2), (2, 2), (4, 1))
 
 
 def hidden_part(x3, ue, gf, bd, g3, weight, bias, col, columns):
@@ -70,7 +70,7 @@
 
 
 def grad_part(g3, ff, f3, weight, col, columns, masks, shares):
-    squares = [jnp.zeros((8, C), F32) for _ in range(columns)]
+    squares = jnp.zeros((8, C), F32)
     for p0, pairs in GROUPS:
         for f, gx in conv(g3, p0, pairs, col, columns, weight):
             for q in range(columns):
@@ -78,9 +78,10 @@
                 if masks[q] is not None:
                     v = v * masks[q]
                 ff[f, q, 8:40, :] = v
-                squares[q] = squares[q] + jnp.sum((v * v).reshape(4, 8, C), axis=0)
+                if shares[q]:
+                    squares = squares + jnp.sum((v * v).reshape(4, 8, C), axis=0)
             spread_rows(ff, f3, (f,), 0, col, columns)
-    return sum(v * share for v, share in zip(squares, shares))
+    return squares
 
 
 def gather_kernel(t_ref, x_ref, u_ref, own_ref, edge_ref, sems):
@@ -97,9 +98,14 @@
         copy.wait()
 
 
-def near_kernel(t_ref, o_ref, p_ref, w_ref, bias_ref,
-                x3, g3, f3, bd, wp, wfp, bias, sq, xf, ue, gf, ff, sems):
+def near_kernel(t_ref, *refs):
     s = lax.rem(t_ref[0], 2)
+    for parity in range(2):
+        pl.when(s == parity)(lambda: near_body(parity, *refs))
+
+
+def near_body(s, o_ref, p_ref, w_ref, bias_ref,
+              x3, g3, f3, bd, wp, wfp, bias, sq, xf, ue, gf, ff, sems):
     pcol = 6 - 6 * s
     copies = (
         pltpu.make_async_copy(w_ref, wp.at[0 : 27 * C, 0:C], sems.at[0]),
@@ -130,15 +136,19 @@
         wfp[k * C : (k + 1) * C, 0:C] = tap
         wfp[(k + 9) * C : (k + 10) * C, C : 2 * C] = tap
     hidden_part(x3, ue, gf, bd, g3, wp, bias[...], 3 - 3 * s, 4)
-    odd = s.astype(F32)
-    sq[...] = grad_part(g3, ff, f3, wfp, 3 - 3 * s, 2, (None, None), (1.0 - odd, odd))
-
-
-def far_kernel(t_ref, o_ref, b_ref, wp, wfp, bias_ref, sq_ref,
-               x3_in, g3_in, f3_in, bd_in, keep_ref, send_ref, x3, g3, f3, bd,
-               xf, ue, gf, ff, cv, gw):
+    sq[...] = grad_part(g3, ff, f3, wfp, 3 - 3 * s, 2, (None, None), (1 - s, s))
+
+
+def far_kernel(t_ref, *refs):
     t = t_ref[0]
     s = lax.rem(t, 2)
+    for parity in range(2):
+        pl.when(s == parity)(lambda: far_body(t, parity, *refs))
+
+
+def far_body(t, s, o_ref, b_ref, wp, wfp, bias_ref, sq_ref,
+             x3_in, g3_in, f3_in, bd_in, keep_ref, send_ref, x3, g3, f3, bd,
+             xf, ue, gf, ff, cv, gw):
     bcol = 6 * s
     zero_rows(xf, 3)
     zero_rows(gf, 3)
@@ -148,11 +158,10 @@
     ue[:, pl.ds(1 + 5 * s, 2)] = b_ref[:, 3:5]
     spread_rows(xf, x3, range(FR), 0, bcol, 3)
     hidden_part(x3, ue, gf, bd, g3, wp, bias_ref[...], 4 * s, 3)
-    odd = s.astype(F32)
-    left_in = jnp.where(t == 0, 0.0, 1.0)
-    right_in = jnp.where(t == TILES - 1, 0.0, 1.0)
+    left_in = None if s else jnp.where(t == 0, 0.0, 1.0)
+    right_in = jnp.where(t == TILES - 1, 0.0, 1.0) if s else None
     squares = sq_ref[...] + grad_part(
-        g3, ff, f3, wfp, 2 * s, 3, (left_in, None, right_in), (odd, 1.0, 1.0 - odd)
+        g3, ff, f3, wfp, 2 * s, 3, (left_in, None, right_in), (s, 1, 1 - s)
     )
     bias_sum = jnp.zeros((8, C), F32)
     for p0, pairs in GROUPS:
@@ -164,27 +173,29 @@
     own = jnp.concatenate([v.astype(F32).reshape(96, C) for v in own], axis=0)
     right = jnp.concatenate([own, cv[...].reshape(FR * 96, C)], axis=0)
     rt = right.T.astype(BF16)
-    for a in range(3):
+    bias_row = jnp.sum(bias_sum, axis=0, keepdims=True)
+    sq_row = jnp.sum(squares, axis=0, keepdims=True)
+    stats = jnp.concatenate([bias_row, bias_row, sq_row, sq_row], axis=0)
+    keep_ref[:, 108:112, :] = jnp.broadcast_to(stats, (16, 4, C))
+    send_ref[:, 108:112, :] = jnp.broadcast_to(stats, (16, 4, C))
+    written = 0
+    for first in range(0, 9, 2):
         cols = []
-        for b in range(3):
+        for ab in range(first, min(first + 2, 9)):
+            a, b = ab // 3, ab % 3
             taps = [f3[(*place(f + a - 1), slice(b, b + 3))] for f in range(FR)]
             taps += [x3[(*place(f + a - 1), slice(2 + b, 5 + b))] for f in range(FR)]
             cols.append(jnp.concatenate([v.reshape(96, 3 * C) for v in taps], axis=0))
         left = jnp.concatenate(cols, axis=1)
         g = jnp.dot(rt, left, preferred_element_type=F32)
-        for k in range(9):
-            gw[(9 * a + k) * C : (9 * a + k + 1) * C, :] = g[:, k * C : (k + 1) * C].T
-    bias_row = jnp.sum(bias_sum, axis=0, keepdims=True)
-    sq_row = jnp.sum(squares, axis=0, keepdims=True)
-    stats = jnp.concatenate([bias_row, bias_row, sq_row, sq_row], axis=0)
-    for core in range(2):
-
-        @pl.when(s == core)
-        def _():
-            for j in range(TILES):
-                ref = keep_ref if j % 2 == core else send_ref
-                ref[j // 2, 0:108, :] = gw[108 * j : 108 * j + 108, :]
-                ref[j // 2, 108:112, :] = stats
+        for k in range(3 * len(cols)):
+            row = (3 * first + k) * C
+            gw[row : row + C, :] = g[:, k * C : (k + 1) * C].T
+        while written < 16 and 216 * (written + 1) <= 3 * C * (first + len(cols)):
+            row = 216 * written
+            keep_ref[written, 0:108, :] = gw[row + 108 * s : row + 108 * s + 108, :]
+            send_ref[written, 0:108, :] = gw[row + 108 - 108 * s : row + 216 - 108 * s, :]
+            written += 1
 
 
 def high_and_low(total):

time: 60.7 us -> 59.8 us (0.985)
  Pallas kernels: 14.1 us -> 13 us
    pallas_call x1, Pallas kernels: 7.3 us -> 6.4 us  [far(): pl.pallas_call(far_kernel, in_specs=[SM] + [VM] * 10, out_specs=[VM] * 6,...]
where the time goes in v3:
time: 59.8 us; the launch traced here: 59.5 us
  blocking collectives  38.6 us (65%)
  Pallas kernels  13 us (22%)
  starting transfers between devices  4.32 us (7%)
  waiting for transfers between devices  2.69 us (4%)
  between operations  0.68 us (1%)
    all_to_all x1, blocking collectives, shards(): lax.all_to_all(total, 'tile', 0, 0, axis_index_groups=groups, tiled=True)  27.2 us
    all_to_all x1, blocking collectives, shards(): everyone = lax.all_to_all(mine, 'clip', 0, 0, tiled=True)  11.4 us
    pallas_call x1, Pallas kernels, far(): pl.pallas_call(far_kernel, in_specs=[SM] + [VM] * 10, out_specs=[VM] * 6,...  6.4 us
    pallas_call x1, Pallas kernels, near(): pl.pallas_call(near_kernel, in_specs=[SM, VM, VM, HB, HB], out_specs=[VM]...  4.62 us
    ppermute x1, starting transfers between devices, shards(): other = lax.ppermute(edge, 'tile', pairs)  3.81 us
    ppermute x1, waiting for transfers between devices, shards(): total = keep + lax.ppermute(send, 'tile', swap)  2.14 us
    pallas_call x1, Pallas kernels, gather(): pl.pallas_call(gather_kernel, in_specs=[SM, HB, HB], out_specs=[VM] * 2,...  1.27 us
  transfers between devices with their start and end apart: 3, of which 2 were waited for; matrix products, arithmetic and copies ran while one was open for 0% of the time, Pallas kernels for 8%

profile of v3, /device:TPU:32, one launch (start us, length us, event | category | flops | bytes accessed | tf_op | source)
XLA Modules:
  0.0 59.5 jit_solution(7896814154957094944)
XLA Ops:
  0.6 1.3 %gather_own.1 = (bf16[2,9,3,32,128]{4,3,2,1,0:T(8,128)(2,1)S(1)}, bf16[9,5,32,128]{3,2,1,0:T(8,128)(2,1)S(1)}) custom-call(s32[1]{0:T(128)} %bitcast.t_ref, bf16[1,9,3,32,128]{4,3,2,1,0:T(8,128)(2,1)} %x_ref.1, bf16[1,9,3,32,128]{4,3,2,1,0:T(8,128)(2,1)} %u_ref.1), custom_call_target="tpu_custom_call" | custom-call | tf_op jit(solution)/shard_map/gather_own/pallas_call | solution.py:237
  1.9 0.1 collective-permute-start.1
  2.0 3.8 %collective-permute-start = (bf16[9,5,32,128]{3,2,1,0:T(8,128)(2,1)S(1)}, bf16[9,5,32,128]{3,2,1,0:T(8,128)(2,1)S(1)}, u32[]{:S(2)}, u32[]{:S(2)}) collective-permute-start(bf16[9,5,32,128]{3,2,1,0:T(8,128)(2,1)S(1)} %get-tuple-element.19), channel_id=1, source_target_pairs={{1,2},{2,1},{3,4},{4,3},{5,6},{6,5},{7,8},{8,7},{9,10},{10,9},{11,... | collective-permute-start | bytes 1105928 | tf_op jit(solution)/shard_map/ppermute | solution.py:308
  5.8 0.0 collective-permute-done.1.refs_1_
  5.8 4.6 %near_columns.1 = (bf16[6,2,9,32,384]{4,3,2,1,0:T(8,128)(2,1)S(1)}, bf16[6,2,7,32,384]{4,3,2,1,0:T(8,128)(2,1)S(1)}, bf16[6,2,5,32,384]{4,3,2,1,0:T(8,128)(2,1)S...) custom-call(s32[1]{0:T(128)} %bitcast.t_ref, ...), custom_call_target="tpu_custom_call" | custom-call | flops 4000000000 | bytes 8000000 | tf_op jit(solution)/shard_map/near_columns/pallas_call | solution.py:249
  10.5 0.5 collective-permute-done.refs_1_
  11.0 6.4 %far_columns.1 = (f32[16,112,128]{2,1,0:T(8,128)S(1)}, f32[16,112,128]{2,1,0:T(8,128)S(1)}, bf16[6,2,9,32,384]{4,3,2,1,0:T(8,128)(2,1)S(1)}, bf16[6,2,7,32,384]{...) custom-call(s32[1]{0:T(128)} %bitcast.t_ref, ...), custom_call_target="tpu_custom_call", output_to_operand_aliasing={{2}: (7, {}), {3}: (8, {}), {4}: (9, {}), {5}: (10, {})} | custom-call | flops 6000000000 | bytes 8000000 | tf_op jit(solution)/shard_map/far_columns/pallas_call | solution.py:277
  17.4 0.4 collective-permute-start.2
  17.8 2.1 %collective-permute-done.2 = f32[16,112,128]{2,1,0:T(8,128)S(1)} collective-permute-done((f32[16,112,128]{2,1,0:T(8,128)S(1)}, f32[16,112,128]{2,1,0:T(8,128)S(1)}, u32[]{:S(2)}, u32[]{:S(2)}) %collective-permute-start.2) | collective-permute-done | bytes 917536 | tf_op jit(solution)/shard_map/ppermute | solution.py:312
  20.0 0.2 fusion
  20.2 27.2 %all_to_all.10.got_ref = bf16[16,112,128]{2,1,0:T(8,128)(2,1)S(1)} all-to-all(bf16[16,112,128]{2,1,0:T(8,128)(2,1)S(1)} %fusion), channel_id=1, replica_groups={{0,2,4,6,8,10,12,14,16,18,20,22,24,26,28,30},{1,3,5,7,9,11,13,15,17,19,..., dimensions={0} | all-to-all | bytes 917504 | tf_op jit(solution)/shard_map/all_to_all | solution.py:318
  47.4 0.1 middle_sum.1
  47.5 11.4 %all_to_all.11.got_ref = bf16[8,112,128]{2,1,0:T(8,128)(2,1)S(1)} all-to-all(bf16[8,112,128]{2,1,0:T(8,128)(2,1)S(1)} %middle_sum.1), channel_id=1, replica_groups=mesh['clip'=8,'tile'=32] {'clip'}, dimensions={0} | all-to-all | bytes 458752 | tf_op jit(solution)/shard_map/all_to_all | solution.py:327
  58.9 0.7 %last_sum.1 = (f32[108,128]{1,0:T(8,128)}, f32[1,128]{1,0:T(1,128)}, f32[1,1]{1,0:T(1,128)}) custom-call(bf16[8,112,128]{2,1,0:T(8,128)(2,1)S(1)} %all_to_all.11.got_ref), custom_call_target="tpu_custom_call" | custom-call | tf_op jit(solution)/shard_map/last_sum/pallas_call | solution.py:328
  (1 shorter events, 0.0 us)
Async XLA Ops:
  1.9 3.9 %collective-permute-start.1 = (bf16[2,9,3,32,128]{4,3,2,1,0:T(8,128)(2,1)S(1)}, bf16[2,9,3,32,128]{4,3,2,1,0:T(8,128)(2,1)S(1)}, u32[]{:S(2)}, u32[]{:S(2)}) collective-permute-start(bf16[2,9,3,32,128]{4,3,2,1,0:T(8,128)(2,1)S(1)} %get-tuple-element.18.refs_0_), channel_id=1, source_target_pairs={{0,1},{1,0},{2,3},{3,2},{4,5},{5,4},{6,7},{7,6},{8,9},{9,8},{10,11... | collective-permute-start | bytes 1327112 | tf_op jit(solution)/shard_map/ppermute | solution.py:309
  2.0 9.0 %collective-permute-start = (bf16[9,5,32,128]{3,2,1,0:T(8,128)(2,1)S(1)}, bf16[9,5,32,128]{3,2,1,0:T(8,128)(2,1)S(1)}, u32[]{:S(2)}, u32[]{:S(2)}) collective-permute-start(bf16[9,5,32,128]{3,2,1,0:T(8,128)(2,1)S(1)} %get-tuple-element.19), channel_id=1, source_target_pairs={{1,2},{2,1},{3,4},{4,3},{5,6},{6,5},{7,8},{8,7},{9,10},{10,9},{11,... | collective-permute-start | bytes 1105928 | tf_op jit(solution)/shard_map/ppermute | solution.py:308
  17.4 2.6 %collective-permute-start.2 = (f32[16,112,128]{2,1,0:T(8,128)S(1)}, f32[16,112,128]{2,1,0:T(8,128)S(1)}, u32[]{:S(2)}, u32[]{:S(2)}) collective-permute-start(f32[16,112,128]{2,1,0:T(8,128)S(1)} %get-tuple-element.29), channel_id=1, source_target_pairs={{0,1},{1,0},{2,3},{3,2},{4,5},{5,4},{6,7},{7,6},{8,9},{9,8},{10,11... | collective-permute-start | bytes 2752520 | tf_op jit(solution)/shard_map/ppermute | solution.py:312

commit v4 on v3

--- a/solution.py
+++ b/solution.py
@@ -286,7 +286,7 @@
             pltpu.VMEM((FR, 3, 48, C), F32),
             pltpu.VMEM((FR, 3, 48, C), F32),
             pltpu.VMEM((FR, 3, ROWS, C), F32),
-            pltpu.VMEM((27 * C, C), F32),
+            pltpu.VMEM((27 * C + 8, C), F32),
         ],
         input_output_aliases={7: 2, 8: 3, 9: 4, 10: 5},
         compiler_params=params(24),

time: 59.8 us -> 59.8 us (level)
  no operation moved by 1% of the time
where the time goes in v4:
time: 59.8 us; the launch traced here: 59.5 us
  blocking collectives  38.6 us (65%)
  Pallas kernels  13 us (22%)
  starting transfers between devices  4.31 us (7%)
  waiting for transfers between devices  2.7 us (5%)
  between operations  0.68 us (1%)
    all_to_all x1, blocking collectives, shards(): lax.all_to_all(total, 'tile', 0, 0, axis_index_groups=groups, tiled=True)  27.2 us
    all_to_all x1, blocking collectives, shards(): everyone = lax.all_to_all(mine, 'clip', 0, 0, tiled=True)  11.4 us
    pallas_call x1, Pallas kernels, far(): pl.pallas_call(far_kernel, in_specs=[SM] + [VM] * 10, out_specs=[VM] * 6,...  6.4 us
    pallas_call x1, Pallas kernels, near(): pl.pallas_call(near_kernel, in_specs=[SM, VM, VM, HB, HB], out_specs=[VM]...  4.62 us
    ppermute x1, starting transfers between devices, shards(): other = lax.ppermute(edge, 'tile', pairs)  3.81 us
    ppermute x1, waiting for transfers between devices, shards(): total = keep + lax.ppermute(send, 'tile', swap)  2.15 us
    pallas_call x1, Pallas kernels, gather(): pl.pallas_call(gather_kernel, in_specs=[SM, HB, HB], out_specs=[VM] * 2,...  1.27 us
  transfers between devices with their start and end apart: 3, of which 2 were waited for; matrix products, arithmetic and copies ran while one was open for 0% of the time, Pallas kernels for 8%

profile of v4, /device:TPU:32, one launch (start us, length us, event | category | flops | bytes accessed | tf_op | source)
XLA Modules:
  0.0 59.5 jit_solution(10887561830336665647)
XLA Ops:
  0.6 1.3 %gather_own.1 = (bf16[2,9,3,32,128]{4,3,2,1,0:T(8,128)(2,1)S(1)}, bf16[9,5,32,128]{3,2,1,0:T(8,128)(2,1)S(1)}) custom-call(s32[1]{0:T(128)} %bitcast.t_ref, bf16[1,9,3,32,128]{4,3,2,1,0:T(8,128)(2,1)} %x_ref.1, bf16[1,9,3,32,128]{4,3,2,1,0:T(8,128)(2,1)} %u_ref.1), custom_call_target="tpu_custom_call" | custom-call | tf_op jit(solution)/shard_map/gather_own/pallas_call | solution.py:237
  1.9 0.1 collective-permute-start.1
  2.0 3.8 %collective-permute-start = (bf16[9,5,32,128]{3,2,1,0:T(8,128)(2,1)S(1)}, bf16[9,5,32,128]{3,2,1,0:T(8,128)(2,1)S(1)}, u32[]{:S(2)}, u32[]{:S(2)}) collective-permute-start(bf16[9,5,32,128]{3,2,1,0:T(8,128)(2,1)S(1)} %get-tuple-element.19), channel_id=1, source_target_pairs={{1,2},{2,1},{3,4},{4,3},{5,6},{6,5},{7,8},{8,7},{9,10},{10,9},{11,... | collective-permute-start | bytes 1105928 | tf_op jit(solution)/shard_map/ppermute | solution.py:308
  5.8 0.0 collective-permute-done.1.refs_1_
  5.8 4.6 %near_columns.1 = (bf16[6,2,9,32,384]{4,3,2,1,0:T(8,128)(2,1)S(1)}, bf16[6,2,7,32,384]{4,3,2,1,0:T(8,128)(2,1)S(1)}, bf16[6,2,5,32,384]{4,3,2,1,0:T(8,128)(2,1)S...) custom-call(s32[1]{0:T(128)} %bitcast.t_ref, ...), custom_call_target="tpu_custom_call" | custom-call | flops 4000000000 | bytes 8000000 | tf_op jit(solution)/shard_map/near_columns/pallas_call | solution.py:249
  10.5 0.5 collective-permute-done.refs_1_
  11.0 6.4 %far_columns.1 = (f32[16,112,128]{2,1,0:T(8,128)S(1)}, f32[16,112,128]{2,1,0:T(8,128)S(1)}, bf16[6,2,9,32,384]{4,3,2,1,0:T(8,128)(2,1)S(1)}, bf16[6,2,7,32,384]{...) custom-call(s32[1]{0:T(128)} %bitcast.t_ref, ...), custom_call_target="tpu_custom_call", output_to_operand_aliasing={{2}: (7, {}), {3}: (8, {}), {4}: (9, {}), {5}: (10, {})} | custom-call | flops 6000000000 | bytes 8000000 | tf_op jit(solution)/shard_map/far_columns/pallas_call | solution.py:277
  17.4 0.4 collective-permute-start.2
  17.8 2.1 %collective-permute-done.2 = f32[16,112,128]{2,1,0:T(8,128)S(1)} collective-permute-done((f32[16,112,128]{2,1,0:T(8,128)S(1)}, f32[16,112,128]{2,1,0:T(8,128)S(1)}, u32[]{:S(2)}, u32[]{:S(2)}) %collective-permute-start.2) | collective-permute-done | bytes 917536 | tf_op jit(solution)/shard_map/ppermute | solution.py:312
  20.0 0.2 fusion
  20.2 27.2 %all_to_all.10.got_ref = bf16[16,112,128]{2,1,0:T(8,128)(2,1)S(1)} all-to-all(bf16[16,112,128]{2,1,0:T(8,128)(2,1)S(1)} %fusion), channel_id=1, replica_groups={{0,2,4,6,8,10,12,14,16,18,20,22,24,26,28,30},{1,3,5,7,9,11,13,15,17,19,..., dimensions={0} | all-to-all | bytes 917504 | tf_op jit(solution)/shard_map/all_to_all | solution.py:318
  47.4 0.1 middle_sum.1
  47.5 11.4 %all_to_all.11.got_ref = bf16[8,112,128]{2,1,0:T(8,128)(2,1)S(1)} all-to-all(bf16[8,112,128]{2,1,0:T(8,128)(2,1)S(1)} %middle_sum.1), channel_id=1, replica_groups=mesh['clip'=8,'tile'=32] {'clip'}, dimensions={0} | all-to-all | bytes 458752 | tf_op jit(solution)/shard_map/all_to_all | solution.py:327
  58.9 0.7 %last_sum.1 = (f32[108,128]{1,0:T(8,128)}, f32[1,128]{1,0:T(1,128)}, f32[1,1]{1,0:T(1,128)}) custom-call(bf16[8,112,128]{2,1,0:T(8,128)(2,1)S(1)} %all_to_all.11.got_ref), custom_call_target="tpu_custom_call" | custom-call | tf_op jit(solution)/shard_map/last_sum/pallas_call | solution.py:328
  (1 shorter events, 0.0 us)
Async XLA Ops:
  1.9 3.9 %collective-permute-start.1 = (bf16[2,9,3,32,128]{4,3,2,1,0:T(8,128)(2,1)S(1)}, bf16[2,9,3,32,128]{4,3,2,1,0:T(8,128)(2,1)S(1)}, u32[]{:S(2)}, u32[]{:S(2)}) collective-permute-start(bf16[2,9,3,32,128]{4,3,2,1,0:T(8,128)(2,1)S(1)} %get-tuple-element.18.refs_0_), channel_id=1, source_target_pairs={{0,1},{1,0},{2,3},{3,2},{4,5},{5,4},{6,7},{7,6},{8,9},{9,8},{10,11... | collective-permute-start | bytes 1327112 | tf_op jit(solution)/shard_map/ppermute | solution.py:309
  2.0 9.0 %collective-permute-start = (bf16[9,5,32,128]{3,2,1,0:T(8,128)(2,1)S(1)}, bf16[9,5,32,128]{3,2,1,0:T(8,128)(2,1)S(1)}, u32[]{:S(2)}, u32[]{:S(2)}) collective-permute-start(bf16[9,5,32,128]{3,2,1,0:T(8,128)(2,1)S(1)} %get-tuple-element.19), channel_id=1, source_target_pairs={{1,2},{2,1},{3,4},{4,3},{5,6},{6,5},{7,8},{8,7},{9,10},{10,9},{11,... | collective-permute-start | bytes 1105928 | tf_op jit(solution)/shard_map/ppermute | solution.py:308
  17.4 2.6 %collective-permute-start.2 = (f32[16,112,128]{2,1,0:T(8,128)S(1)}, f32[16,112,128]{2,1,0:T(8,128)S(1)}, u32[]{:S(2)}, u32[]{:S(2)}) collective-permute-start(f32[16,112,128]{2,1,0:T(8,128)S(1)} %get-tuple-element.29), channel_id=1, source_target_pairs={{0,1},{1,0},{2,3},{3,2},{4,5},{5,4},{6,7},{7,6},{8,9},{9,8},{10,11... | collective-permute-start | bytes 2752520 | tf_op jit(solution)/shard_map/ppermute | solution.py:312

commit v5 on v4

--- a/solution.py
+++ b/solution.py
@@ -98,15 +98,7 @@
         copy.wait()
 
 
-def near_kernel(t_ref, *refs):
-    s = lax.rem(t_ref[0], 2)
-    for parity in range(2):
-        pl.when(s == parity)(lambda: near_body(parity, *refs))
-
-
-def near_body(s, o_ref, p_ref, w_ref, bias_ref,
-              x3, g3, f3, bd, wp, wfp, bias, sq, xf, ue, gf, ff, sems):
-    pcol = 6 - 6 * s
+def own_kernel(o_ref, w_ref, bias_ref, x3, g3, f3, wp, wfp, bias, xf, sems):
     copies = (
         pltpu.make_async_copy(w_ref, wp.at[0 : 27 * C, 0:C], sems.at[0]),
         pltpu.make_async_copy(w_ref, wp.at[9 * C : 36 * C, C : 2 * C], sems.at[1]),
@@ -117,24 +109,36 @@
     for m in (wp, wfp):
         m[27 * C : 36 * C, 0:C] = jnp.zeros((9 * C, C), BF16)
         m[0 : 9 * C, C : 2 * C] = jnp.zeros((9 * C, C), BF16)
-    zero_rows(xf, 6)
-    zero_rows(gf, 4)
-    zero_rows(ff, 2)
+    zero_rows(xf, 3)
     zero_frames(x3, 9)
     zero_frames(g3, 7)
     zero_frames(f3, 5)
-    xf[:, 0:3, 8:40, :] = o_ref[0].astype(F32)
-    xf[:, 3:6, 8:40, :] = p_ref[0].astype(F32)
-    ue[:, 3:6] = o_ref[1]
-    ue[:, pl.ds(pcol, 3)] = p_ref[1]
+    xf[:, :, 8:40, :] = o_ref[0].astype(F32)
     spread_rows(xf, x3, range(FR), 0, 3, 3)
-    spread_rows(xf, x3, range(FR), 3, pcol, 3)
     for copy in copies:
         copy.wait()
     for k in range(27):
         tap = wp[(26 - k) * C : (27 - k) * C, 0:C].astype(F32).T.astype(BF16)
         wfp[k * C : (k + 1) * C, 0:C] = tap
         wfp[(k + 9) * C : (k + 10) * C, C : 2 * C] = tap
+
+
+def near_kernel(t_ref, *refs):
+    s = lax.rem(t_ref[0], 2)
+    for parity in range(2):
+        pl.when(s == parity)(lambda: near_body(parity, *refs))
+
+
+def near_body(s, o_ref, p_ref, wp, wfp, bias, x3_in, g3_in, f3_in,
+              x3, g3, f3, bd, sq, xf, ue, gf, ff):
+    pcol = 6 - 6 * s
+    zero_rows(xf, 3)
+    zero_rows(gf, 4)
+    zero_rows(ff, 2)
+    xf[:, :, 8:40, :] = p_ref[0].astype(F32)
+    ue[:, 3:6] = o_ref[1]
+    ue[:, pl.ds(pcol, 3)] = p_ref[1]
+    spread_rows(xf, x3, range(FR), 0, pcol, 3)
     hidden_part(x3, ue, gf, bd, g3, wp, bias[...], 3 - 3 * s, 4)
     sq[...] = grad_part(g3, ff, f3, wfp, 3 - 3 * s, 2, (None, None), (1 - s, s))
 
@@ -245,32 +249,44 @@
     )(t, x, u)
 
 
-def near(t, own, p, w, bias):
+def prepare(own, w, bias):
     return pl.pallas_call(
-        near_kernel,
-        in_specs=[SM, VM, VM, HB, HB],
-        out_specs=[VM] * 8,
+        own_kernel,
+        in_specs=[VM, HB, HB],
+        out_specs=[VM] * 6,
         out_shape=[
             shape(BF16, 6, 2, 9, ROWS, 3 * C),
             shape(BF16, 6, 2, 7, ROWS, 3 * C),
             shape(BF16, 6, 2, 5, ROWS, 3 * C),
-            shape(F32, FR, 7, ROWS, C),
             shape(BF16, 36 * C, 2 * C),
             shape(BF16, 36 * C, 2 * C),
             shape(F32, 1, C),
-            shape(F32, 8, C),
         ],
+        scratch_shapes=[pltpu.VMEM((FR, 3, 48, C), F32), pltpu.SemaphoreType.DMA((3,))],
+        compiler_params=params(16),
+        cost_estimate=pl.CostEstimate(flops=1_000_000_000, bytes_accessed=8_000_000, transcendentals=0),
+        name="own_columns",
+    )(own, w, bias)
+
+
+def near(t, own, p, wp, wfp, bias, x3, g3, f3):
+    return pl.pallas_call(
+        near_kernel,
+        in_specs=[SM] + [VM] * 8,
+        out_specs=[VM] * 5,
+        out_shape=[shape(v.dtype, *v.shape) for v in (x3, g3, f3)]
+        + [shape(F32, FR, 7, ROWS, C), shape(F32, 8, C)],
         scratch_shapes=[
-            pltpu.VMEM((FR, 6, 48, C), F32),
+            pltpu.VMEM((FR, 3, 48, C), F32),
             pltpu.VMEM((FR, 9, ROWS, C), BF16),
             pltpu.VMEM((FR, 4, 48, C), F32),
             pltpu.VMEM((FR, 2, 48, C), F32),
-            pltpu.SemaphoreType.DMA((3,)),
         ],
+        input_output_aliases={6: 0, 7: 1, 8: 2},
         compiler_params=params(24),
         cost_estimate=pl.CostEstimate(flops=4_000_000_000, bytes_accessed=8_000_000, transcendentals=0),
         name="near_columns",
-    )(t, own, p, w, bias)
+    )(t, own, p, wp, wfp, bias, x3, g3, f3)
 
 
 def far(t, own, b, wp, wfp, bias, sq, x3, g3, f3, bd):
@@ -307,7 +323,8 @@
     own, edge = gather(t, in_hbm(clip_features), in_hbm(upstream))
     other = lax.ppermute(edge, "tile", pairs)
     partner = lax.ppermute(own, "tile", swap)
-    x3, g3, f3, bd, wp, wfp, bias, sq = near(t, own, partner, in_hbm(w), in_hbm(bias))
+    x3, g3, f3, wp, wfp, bias = prepare(own, in_hbm(w), in_hbm(bias))
+    x3, g3, f3, bd, sq = near(t, own, partner, wp, wfp, bias, x3, g3, f3)
     keep, send = far(t, own, other, wp, wfp, bias, sq, x3, g3, f3, bd)
     total = keep + lax.ppermute(send, "tile", swap)
     row = lax.broadcasted_iota(jnp.int32, (1, BLOCK, 1), 1)

time: 59.8 us -> 59.9 us (level)
  Pallas kernels: 13 us -> 13.6 us
    pallas_call x1 -> x2, Pallas kernels: 4.62 us -> 5.04 us  [the longest x1 3.15 us: near(): pl.pallas_call(near_kernel, in_specs=[SM] + [VM] * 8, out_specs=[VM] * 5,...]
where the time goes in v5:
time: 59.9 us; the launch traced here: 59.7 us
  blocking collectives  38.6 us (64%)
  Pallas kernels  13.6 us (23%)
  starting transfers between devices  4.12 us (7%)
  waiting for transfers between devices  2.46 us (4%)
  between operations  0.7 us (1%)
    all_to_all x1, blocking collectives, shards(): lax.all_to_all(total, 'tile', 0, 0, axis_index_groups=groups, tiled=True)  27.2 us
    all_to_all x1, blocking collectives, shards(): everyone = lax.all_to_all(mine, 'clip', 0, 0, tiled=True)  11.4 us
    pallas_call x1, Pallas kernels, far(): pl.pallas_call(far_kernel, in_specs=[SM] + [VM] * 10, out_specs=[VM] * 6,...  6.54 us
    ppermute x1, starting transfers between devices, shards(): other = lax.ppermute(edge, 'tile', pairs)  3.81 us
    pallas_call x1, Pallas kernels, near(): pl.pallas_call(near_kernel, in_specs=[SM] + [VM] * 8, out_specs=[VM] * 5,...  3.15 us
    ppermute x1, waiting for transfers between devices, shards(): total = keep + lax.ppermute(send, 'tile', swap)  2.34 us
    pallas_call x1, Pallas kernels, prepare(): pl.pallas_call(own_kernel, in_specs=[VM, HB, HB], out_specs=[VM] * 6, out...  1.88 us
    pallas_call x1, Pallas kernels, gather(): pl.pallas_call(gather_kernel, in_specs=[SM, HB, HB], out_specs=[VM] * 2,...  1.27 us
  transfers between devices with their start and end apart: 3, of which 2 were waited for; matrix products, arithmetic and copies ran while one was open for 0% of the time, Pallas kernels for 8%

profile of v5, /device:TPU:32, one launch (start us, length us, event | category | flops | bytes accessed | tf_op | source)
XLA Modules:
  0.0 59.7 jit_solution(9380929782271670201)
XLA Ops:
  0.6 1.3 %gather_own.1 = (bf16[2,9,3,32,128]{4,3,2,1,0:T(8,128)(2,1)S(1)}, bf16[9,5,32,128]{3,2,1,0:T(8,128)(2,1)S(1)}) custom-call(s32[1]{0:T(128)} %bitcast.t_ref, bf16[1,9,3,32,128]{4,3,2,1,0:T(8,128)(2,1)} %x_ref.1, bf16[1,9,3,32,128]{4,3,2,1,0:T(8,128)(2,1)} %u_ref.1), custom_call_target="tpu_custom_call" | custom-call | tf_op jit(solution)/shard_map/gather_own/pallas_call | solution.py:241
  1.9 0.1 collective-permute-start.1
  2.0 3.8 %collective-permute-start = (bf16[9,5,32,128]{3,2,1,0:T(8,128)(2,1)S(1)}, bf16[9,5,32,128]{3,2,1,0:T(8,128)(2,1)S(1)}, u32[]{:S(2)}, u32[]{:S(2)}) collective-permute-start(bf16[9,5,32,128]{3,2,1,0:T(8,128)(2,1)S(1)} %get-tuple-element.22), channel_id=1, source_target_pairs={{1,2},{2,1},{3,4},{4,3},{5,6},{6,5},{7,8},{8,7},{9,10},{10,9},{11,... | collective-permute-start | bytes 1105928 | tf_op jit(solution)/shard_map/ppermute | solution.py:324
  5.8 1.9 %own_columns.1 = (bf16[6,2,9,32,384]{4,3,2,1,0:T(8,128)(2,1)S(1)}, bf16[6,2,7,32,384]{4,3,2,1,0:T(8,128)(2,1)S(1)}, bf16[6,2,5,32,384]{4,3,2,1,0:T(8,128)(2,1)S(...) custom-call(bf16[2,9,3,32,128]{4,3,2,1,0:T(8,128)(2,1)S(1)} %get-tuple-element.21.o_ref.refs_, ...), custom_call_target="tpu_custom_call" | custom-call | flops 1000000000 | bytes 8000000 | tf_op jit(solution)/shard_map/own_columns/pallas_call | solution.py:253
  7.7 0.0 collective-permute-done.1.refs_1_
  7.7 3.2 %near_columns.1 = (bf16[6,2,9,32,384]{4,3,2,1,0:T(8,128)(2,1)S(1)}, bf16[6,2,7,32,384]{4,3,2,1,0:T(8,128)(2,1)S(1)}, bf16[6,2,5,32,384]{4,3,2,1,0:T(8,128)(2,1)S...) custom-call(s32[1]{0:T(128)} %bitcast.t_ref, ...), custom_call_target="tpu_custom_call", output_to_operand_aliasing={{0}: (6, {}), {1}: (7, {}), {2}: (8, {})} | custom-call | flops 4000000000 | bytes 8000000 | tf_op jit(solution)/shard_map/near_columns/pallas_call | solution.py:273
  10.9 0.1 collective-permute-done.refs_1_
  11.0 6.5 %far_columns.1 = (f32[16,112,128]{2,1,0:T(8,128)S(1)}, f32[16,112,128]{2,1,0:T(8,128)S(1)}, bf16[6,2,9,32,384]{4,3,2,1,0:T(8,128)(2,1)S(1)}, bf16[6,2,7,32,384]{...) custom-call(s32[1]{0:T(128)} %bitcast.t_ref, ...), custom_call_target="tpu_custom_call", output_to_operand_aliasing={{2}: (7, {}), {3}: (8, {}), {4}: (9, {}), {5}: (10, {})} | custom-call | flops 6000000000 | bytes 8000000 | tf_op jit(solution)/shard_map/far_columns/pallas_call | solution.py:293
  17.6 0.2 collective-permute-start.2
  17.8 2.3 %collective-permute-done.2 = f32[16,112,128]{2,1,0:T(8,128)S(1)} collective-permute-done((f32[16,112,128]{2,1,0:T(8,128)S(1)}, f32[16,112,128]{2,1,0:T(8,128)S(1)}, u32[]{:S(2)}, u32[]{:S(2)}) %collective-permute-start.2) | collective-permute-done | bytes 917536 | tf_op jit(solution)/shard_map/ppermute | solution.py:329
  20.1 0.2 fusion
  20.3 27.2 %all_to_all.10.got_ref = bf16[16,112,128]{2,1,0:T(8,128)(2,1)S(1)} all-to-all(bf16[16,112,128]{2,1,0:T(8,128)(2,1)S(1)} %fusion), channel_id=1, replica_groups={{0,2,4,6,8,10,12,14,16,18,20,22,24,26,28,30},{1,3,5,7,9,11,13,15,17,19,..., dimensions={0} | all-to-all | bytes 917504 | tf_op jit(solution)/shard_map/all_to_all | solution.py:335
  47.6 0.1 middle_sum.1
  47.6 11.4 %all_to_all.11.got_ref = bf16[8,112,128]{2,1,0:T(8,128)(2,1)S(1)} all-to-all(bf16[8,112,128]{2,1,0:T(8,128)(2,1)S(1)} %middle_sum.1), channel_id=1, replica_groups=mesh['clip'=8,'tile'=32] {'clip'}, dimensions={0} | all-to-all | bytes 458752 | tf_op jit(solution)/shard_map/all_to_all | solution.py:344
  59.0 0.7 %last_sum.1 = (f32[108,128]{1,0:T(8,128)}, f32[1,128]{1,0:T(1,128)}, f32[1,1]{1,0:T(1,128)}) custom-call(bf16[8,112,128]{2,1,0:T(8,128)(2,1)S(1)} %all_to_all.11.got_ref), custom_call_target="tpu_custom_call" | custom-call | tf_op jit(solution)/shard_map/last_sum/pallas_call | solution.py:345
  (1 shorter events, 0.0 us)
Async XLA Ops:
  1.9 5.8 %collective-permute-start.1 = (bf16[2,9,3,32,128]{4,3,2,1,0:T(8,128)(2,1)S(1)}, bf16[2,9,3,32,128]{4,3,2,1,0:T(8,128)(2,1)S(1)}, u32[]{:S(2)}, u32[]{:S(2)}) collective-permute-start(bf16[2,9,3,32,128]{4,3,2,1,0:T(8,128)(2,1)S(1)} %get-tuple-element.21.o_ref.refs_0_), channel_id=1, source_target_pairs={{0,1},{1,0},{2,3},{3,2},{4,5},{5,4},{6,7},{7,6},{8,9},{9,8},{10,11... | collective-permute-start | bytes 1327112 | tf_op jit(solution)/shard_map/ppermute | solution.py:325
  2.0 9.0 %collective-permute-start = (bf16[9,5,32,128]{3,2,1,0:T(8,128)(2,1)S(1)}, bf16[9,5,32,128]{3,2,1,0:T(8,128)(2,1)S(1)}, u32[]{:S(2)}, u32[]{:S(2)}) collective-permute-start(bf16[9,5,32,128]{3,2,1,0:T(8,128)(2,1)S(1)} %get-tuple-element.22), channel_id=1, source_target_pairs={{1,2},{2,1},{3,4},{4,3},{5,6},{6,5},{7,8},{8,7},{9,10},{10,9},{11,... | collective-permute-start | bytes 1105928 | tf_op jit(solution)/shard_map/ppermute | solution.py:324
  17.6 2.6 %collective-permute-start.2 = (f32[16,112,128]{2,1,0:T(8,128)S(1)}, f32[16,112,128]{2,1,0:T(8,128)S(1)}, u32[]{:S(2)}, u32[]{:S(2)}) collective-permute-start(f32[16,112,128]{2,1,0:T(8,128)S(1)} %get-tuple-element.35), channel_id=1, source_target_pairs={{0,1},{1,0},{2,3},{3,2},{4,5},{5,4},{6,7},{7,6},{8,9},{9,8},{10,11... | collective-permute-start | bytes 2752520 | tf_op jit(solution)/shard_map/ppermute | solution.py:329
